TPU v7x, 256 devices: a whole 4x4x8 slice. The times are simulated.
256 devices in a mesh: section: 16 (over y, x_hi, core), ctx: 16 (over z, x_lo).
Axes of the slice: x: 4 (x_hi: 2, x_lo: 2; x = x_hi * 2 + x_lo), y: 4, z: 8, core: 2. Of those that a mesh axis runs over, the one named last changes fastest.
Arguments:
- section_inputs: bfloat16 [16, 1792, 2048], P('section', 'ctx'), may hold values from -3 to 3
- saved_inputs: bfloat16 [16, 1792, 2048], P('section', 'ctx'), may hold values from -3 to 3
- output_grads: bfloat16 [16, 1792, 2048], P('section', 'ctx'), may hold values from -6 to 6
- token_positions: int32 [1792], P('ctx'), may hold values from 0 to 1791, each once
- norm_gain: float32 [16, 2048], P('section'), may hold values from 0.7 to 6
- query_weight: bfloat16 [16, 2048, 2048], P('section', 'ctx'), may hold values from -0.13258252 to 0.13258252
- keyval_weight: bfloat16 [16, 2048, 1024], P('section', 'ctx'), may hold values from -0.13258252 to 0.13258252
- output_weight: bfloat16 [16, 2048, 2048], P('section'), may hold values from -0.125 to 0.125
Outputs:
- next_inputs: bfloat16 [16, 1792, 2048], P('section', 'ctx')
- input_grads: bfloat16 [16, 1792, 2048], P('section', 'ctx')
Inputs may be any that keep to these rules, and one draw needn't show every extreme that they name: `token_positions`: each position of the sequence once.
All inputs are finite; a program needn't handle non-finite values.
Results may differ from a plain program's by a relative error of at most 0.04.
The roundings to bfloat16 on the way count: a program that leaves them out, or rounds other values in their place, can miss the bound.
Values may be sent and summed in bfloat16 or wider, within the bound.
A program may use at most 192 MiB of HBM per device.

v0:
```python
import jax
import jax.numpy as jnp
from jax import lax
from jax.sharding import Mesh
from jax.sharding import PartitionSpec as P

HEAD_DIM = 128
CTX = ("ctx_0", "ctx_1")


norm_eps = 1e-05
rope_base = 500000.0


def copy_for_each(shard, axis):
    devices = lax.axis_size(axis)
    return lax.all_to_all(
        jnp.broadcast_to(shard[None], (devices, *shard.shape)), axis, 0, 0, tiled=True
    )


def joined_along(parts, dim):
    dims = list(parts.shape[1:])
    dims[dim] *= parts.shape[0]
    return jnp.moveaxis(parts, 0, dim).reshape(dims)


def gathered_copies(shard, axis, dim):
    parts = copy_for_each(shard, axis)
    return joined_along(parts, dim)


def side_by_side(arrays, axis, dim, along):
    widths = [a.shape[along] for a in arrays]
    both = jnp.concatenate(arrays, axis=along)
    filled = lax.all_gather(both, axis, axis=dim, tiled=True)
    return tuple(jnp.split(filled, [sum(widths[:k]) for k in range(1, len(widths))], axis=along))


def from_behind(block, axis, distance):
    devices = range(lax.axis_size(axis))
    route = [((i - distance) % len(devices), i) for i in devices]
    return lax.ppermute(block, axis, route)


def summed_rows(shard, axes, dim):
    for axis in axes:
        shard = lax.psum_scatter(shard, axis, scatter_dimension=dim, tiled=True)
    return shard


def rotate(matrix, positions):
    half_dim = matrix.shape[-1] // 2
    frequency = rope_base ** (-2.0 * jnp.arange(half_dim, dtype=jnp.float32) / matrix.shape[-1])
    angles = positions.astype(jnp.float32)[:, None] * frequency[None, :]
    cos_table = jnp.cos(angles)[:, None, :]
    sin_table = jnp.sin(angles)[:, None, :]
    leading = matrix[..., :half_dim]
    trailing = matrix[..., half_dim:]
    return jnp.concatenate(
        [leading * cos_table - trailing * sin_table, trailing * cos_table + leading * sin_table],
        axis=-1,
    )


def project(tokens, gain, query_matrix, keyval_matrix, positions):
    widened = tokens.astype(jnp.float32)
    inverse = lax.rsqrt(jnp.mean(widened * widened, axis=-1, keepdims=True) + norm_eps)
    normed = (widened * inverse * gain[None, :]).astype(jnp.bfloat16)
    row_count = tokens.shape[0]
    query_full = jnp.dot(normed, query_matrix, preferred_element_type=jnp.float32)
    keyval_full = jnp.dot(normed, keyval_matrix, preferred_element_type=jnp.float32)
    queries = rotate(query_full.reshape(row_count, -1, HEAD_DIM), positions).astype(jnp.bfloat16)
    paired = keyval_full.reshape(row_count, 2, -1, HEAD_DIM)
    key_rows = rotate(paired[:, 0], positions).astype(jnp.bfloat16)
    value_rows = paired[:, 1].astype(jnp.bfloat16)
    return (queries, key_rows, value_rows)


def attend(queries, key_wide, value_wide, query_pos, key_pos, narrow):
    row_count = queries.shape[0]
    kv_count = key_wide.shape[1]
    head_size = queries.shape[2]
    group_size = queries.shape[1] // kv_count
    grouped = jnp.moveaxis(queries.reshape(row_count, kv_count, group_size, head_size), 1, 0)
    key_heads = jnp.moveaxis(key_wide, 1, 0)
    value_heads = jnp.moveaxis(value_wide, 1, 0)
    visible = (key_pos[None, :] <= query_pos[:, None])[None]

    def one_head(block):
        query_block, key_block, value_block = block
        scores = jnp.einsum(
            "rgd,sd->grs", query_block, key_block, preferred_element_type=jnp.float32
        ) * head_size ** (-0.5)
        masked = jnp.where(visible, scores, -1e30)
        row_max = lax.stop_gradient(jnp.max(masked, axis=-1, keepdims=True))
        numerators = jnp.where(visible, jnp.exp(masked - row_max), 0.0)
        totals = jnp.sum(numerators, axis=-1)
        if narrow:
            rounded = numerators.astype(jnp.bfloat16)
        else:
            rounded = lax.optimization_barrier(numerators.astype(jnp.bfloat16)).astype(jnp.float32)
        summed = jnp.einsum("grs,sd->rgd", rounded, value_block, preferred_element_type=jnp.float32)
        return summed / jnp.transpose(totals, (1, 0))[..., None]

    averaged = lax.map(one_head, (grouped, key_heads, value_heads))
    return jnp.moveaxis(averaged, 0, 1).reshape(row_count, -1).astype(jnp.bfloat16)


def finish(tokens, mixed, output_matrix):
    return (
        tokens.astype(jnp.float32)
        + jnp.dot(mixed, output_matrix, preferred_element_type=jnp.float32)
    ).astype(jnp.bfloat16)


def shards(
    section_inputs,
    saved_inputs,
    output_grads,
    token_positions,
    norm_gain,
    query_weight,
    keyval_weight,
    output_weight,
):
    key_positions = gathered_copies(token_positions, CTX, 0)
    full_query, full_keyval = side_by_side((query_weight[0], keyval_weight[0]), CTX, 0, 1)
    full_output = output_weight[0]
    gain = norm_gain[0]
    forward_tokens = section_inputs[0]
    saved_tokens = saved_inputs[0]
    upstream = output_grads[0]

    def projector(tokens):
        return project(tokens, gain, full_query, full_keyval, token_positions)

    def attention_wide(queries, key_wide, value_wide):
        return attend(queries, key_wide, value_wide, token_positions, key_positions, False)

    def finishing(tokens, mixed):
        return finish(tokens, mixed, full_output)

    forward_queries, forward_keys, forward_values = projector(forward_tokens)
    (backward_queries, backward_keys, backward_values), back_project = jax.vjp(
        projector, saved_tokens
    )
    forward_keyset, forward_valueset, backward_keyset, backward_valueset = side_by_side(
        (forward_keys, forward_values, backward_keys, backward_values), CTX, 0, 1
    )
    mixed = attend(
        forward_queries, forward_keyset, forward_valueset, token_positions, key_positions, True
    )
    produced = finishing(forward_tokens, mixed)
    sent_on = from_behind(produced[None], "section", 1)
    mixed, back_attend = jax.vjp(
        attention_wide,
        backward_queries.astype(jnp.float32),
        backward_keyset.astype(jnp.float32),
        backward_valueset.astype(jnp.float32),
    )
    produced, back_finish = jax.vjp(finishing, saved_tokens, mixed)
    residual_grad, mixed_grad = back_finish(upstream)
    query_grad, key_partial, value_partial = back_attend(mixed_grad)
    key_grads = summed_rows(key_partial.astype(jnp.bfloat16), CTX, 0).astype(jnp.float32)
    value_grads = summed_rows(value_partial.astype(jnp.bfloat16), CTX, 0).astype(jnp.float32)
    (project_grad,) = back_project(
        (
            query_grad.astype(jnp.bfloat16),
            key_grads.astype(jnp.bfloat16),
            value_grads.astype(jnp.bfloat16),
        )
    )
    sent_back = from_behind((residual_grad + project_grad)[None], "section", -1)
    return (sent_on, sent_back)


def solution(mesh):
    torus = Mesh(mesh.devices.reshape(mesh.shape["section"], 8, 2), ("section", "ctx_0", "ctx_1"))
    placed = (
        P("section", CTX, None),
        P("section", CTX, None),
        P("section", CTX, None),
        P(CTX),
        P("section", None),
        P("section", CTX, None),
        P("section", CTX, None),
        P("section", None, None),
    )
    return jax.shard_map(
        shards,
        mesh=torus,
        in_specs=placed,
        out_specs=(P("section", CTX, None), P("section", CTX, None)),
        check_vma=False,
    )
```

profile of v0, /device:TPU:1, one launch (start us, length us, event | category | flops | bytes accessed | tf_op | source)
XLA Modules:
  0.0 716.7 jit_solution(4608696759107310912)
XLA Ops:
  12.8 267.3 %all-gather.3.cloned.1.call-done = bf16[2048,3072]{1,0:T(8,128)(2,1)} async-done(((bf16[128,3072]{1,0:T(8,128)(2,1)}), bf16[2048,3072]{1,0:T(8,128)(2,1)}) %all-gather.3.cloned.1.call-update) | async-done | bytes 12582928 | tf_op jit(solution)/shard_map/all_gather | solution.py:36
  280.1 4.6 slice_bitcast_fusion.1
  284.7 6.6 copy.17
  291.4 3.8 fusion.193
  298.6 9.4 %all-to-all-start = ((s32[16,1,112]{2,1,0:T(1,128)}), s32[16,1,112]{2,1,0:T(1,128)S(1)}, u32[]{:S(2)}, u32[]{:S(2)}) async-start(s32[16,1,112]{2,1,0:T(1,128)} %broadcast_in_dim.184), calls=%async_computation | async-start | bytes 16384 | tf_op jit(solution)/shard_map/all_to_all | solution.py:17
  308.0 6.2 fusion.162
  318.3 8.3 %slice_bitcast_fusion = bf16[2048,2048]{0,1:T(8,128)(2,1)} fusion(bf16[2048,3072]{1,0:T(8,128)(2,1)} %all-gather.3.cloned.1.call-done), kind=kLoop, calls=%fused_computation.110 | loop fusion | bytes 16777216 | tf_op jit(solution)/shard_map/dot_general | solution.py:71
  326.6 12.4 %copy.18 = bf16[2048,2048]{1,0:T(8,128)(2,1)} copy(bf16[2048,2048]{0,1:T(8,128)(2,1)} %slice_bitcast_fusion) | data formatting | bytes 16777216 | tf_op jit(solution)/shard_map/dot_general | solution.py:71
  339.0 6.3 fusion.197
  346.7 115.0 %all-gather.5.cloned.1.call-done = bf16[1792,16,128]{2,0,1:T(8,128)(2,1)} async-done(((bf16[112,16,128]{2,0,1:T(8,128)(2,1)}), bf16[1792,16,128]{2,0,1:T(8,128)(2,1)}) %all-gather.5.cloned.1.call-update) | async-done | bytes 7340048 | tf_op jit(solution)/shard_map/all_gather | solution.py:36
  461.6 6.2 convert_bitcast_fusion
  467.8 43.3 %while.56 = (s32[]{:T(128)}, f32[4,4,112,1792]{3,2,1,0:T(8,128)}, bf16[4,4,112,1792]{3,2,1,0:T(8,128)(2,1)}, f32[4,112,4,1]{1,3,2,0:T(1,128)S(1)}, f32[4,112,4,1...) while((s32[]{:T(128)}, f32[4,4,112,1792]{3,2,1,0:T(8,128)}, ...), condition=%wide.region_9.10_spmd.clone.clone, body=%wide.region_6.9_spmd.clone.sunk.clone | while | flops 416664192 | bytes 74129576 | solution.py:106
  467.8 3.9 bitcast_dynamic-update-slice_fusion.3
  478.6 4.0 bitcast_dynamic-update-slice_fusion.3
  489.5 4.0 bitcast_dynamic-update-slice_fusion.3
  500.2 4.0 bitcast_dynamic-update-slice_fusion.3
  512.8 51.4 %while.57 = (s32[]{:T(128)}, bf16[4,112,4,128]{3,1,2,0:T(8,128)(2,1)S(1)}, bf16[4,1792,128]{2,1,0:T(8,128)(2,1)}, bf16[4,1792,128]{2,1,0:T(8,128)(2,1)S(1)}, f32...) while((s32[]{:T(128)}, ...), condition=%wide.region_12.13_spmd.clone.clone, body=%wide.region_10.12_spmd.clone.sunk.clone | while | flops 832004096 | bytes 16256409 | solution.py:106
  519.4 3.8 fusion.302
  532.2 3.8 fusion.302
  545.1 3.8 fusion.302
  558.0 3.8 fusion.302
  565.8 6.2 fusion.200
  574.3 28.9 %reduce-scatter.9.cloned.1.call-done = bf16[224,4,128]{2,0,1:T(8,128)(2,1)} async-done(((bf16[1792,4,128]{2,0,1:T(8,128)(2,1)}), bf16[224,4,128]{2,0,1:T(8,128)(2,1)}) %reduce-scatter.9.cloned.1.call-update) | async-done | bytes 229392 | tf_op jit(solution)/shard_map/reduce_scatter | solution.py:48
  603.2 20.3 %while.55 = (s32[]{:T(128)}, bf16[4,112,4,128]{3,1,2,0:T(8,128)(2,1)S(1)}, bf16[4,1792,128]{2,1,0:T(8,128)(2,1)}, bf16[4,1792,128]{2,1,0:T(8,128)(2,1)S(1)}, bf1...) while((s32[]{:T(128)}, ...), condition=%wide.region_5.6_spmd.clone.clone, body=%wide.region_2.5_spmd.clone.sunk.clone | while | flops 624852928 | bytes 2853141 | solution.py:106
  624.1 21.7 %reduce-scatter.5.cloned.1.call-done = bf16[224,4,128]{2,0,1:T(8,128)(2,1)} async-done(((bf16[1792,4,128]{2,0,1:T(8,128)(2,1)}), bf16[224,4,128]{2,0,1:T(8,128)(2,1)}) %reduce-scatter.5.cloned.1.call-update) | async-done | bytes 229392 | tf_op jit(solution)/shard_map/reduce_scatter | solution.py:48
  645.8 5.5 fusion.165
  651.3 7.4 %collective-permute-start = (bf16[1,112,2048]{2,1,0:T(8,128)(2,1)}, bf16[1,112,2048]{2,1,0:T(8,128)(2,1)S(1)}, u32[]{:S(2)}, u32[]{:S(2)}) collective-permute-start(bf16[1,112,2048]{2,1,0:T(8,128)(2,1)} %fusion.165), channel_id=1, source_target_pairs={{240,0},{0,16},{16,32},{32,48},{48,64},{64,80},{80,96},{96,112},{1... | collective-permute-start | bytes 1376264 | tf_op jit(solution)/shard_map/ppermute | solution.py:43
  658.7 9.9 %reduce-scatter.11.cloned.1.call-done = bf16[112,4,128]{2,0,1:T(8,128)(2,1)} async-done(((bf16[224,4,128]{2,0,1:T(8,128)(2,1)}), bf16[112,4,128]{2,0,1:T(8,128)(2,1)}) %reduce-scatter.11.cloned.1.call-update) | async-done | bytes 114704 | tf_op jit(solution)/shard_map/reduce_scatter | solution.py:48
  669.8 17.2 %reduce-scatter.7.cloned.1.call-done = bf16[112,4,128]{2,0,1:T(8,128)(2,1)} async-done(((bf16[224,4,128]{2,0,1:T(8,128)(2,1)}), bf16[112,4,128]{2,0,1:T(8,128)(2,1)}) %reduce-scatter.7.cloned.1.call-update) | async-done | bytes 114704 | tf_op jit(solution)/shard_map/reduce_scatter | solution.py:48
  688.2 3.8 fusion.156
  692.0 6.4 fusion.182
  699.7 8.6 %collective-permute-done.1 = bf16[1,112,2048]{2,1,0:T(8,128)(2,1)S(1)} collective-permute-done((bf16[1,112,2048]{2,1,0:T(8,128)(2,1)S(1)}, bf16[1,112,2048]{2,1,0:T(8,128)(2,1)S(1)}, u32[]{:S(2)}, u32[]{:S(2)}) %collective-permute-start.1) | collective-permute-done | bytes 458784 | tf_op jit(solution)/shard_map/ppermute | solution.py:43
  (182 shorter events, 108.9 us)
Async XLA Ops:
  7.2 272.9 %all-gather.3.cloned.1.call-start = ((), (), s32[]{:S(2)}) async-start(), calls=%async_computation.5 | async-start | bytes 13369344 | tf_op jit(solution)/shard_map/all_gather | solution.py:36
  9.3 452.3 %all-gather.5.cloned.1.call-start = ((), (), s32[]{:S(2)}) async-start(), calls=%async_computation.6 | async-start | bytes 7798784 | tf_op jit(solution)/shard_map/all_gather | solution.py:36
  12.5 326.5 %copy-start.17 = (f32[112]{0:T(128)}, f32[112]{0:T(128)S(1)}, u32[]{:S(2)}) copy-start(f32[112]{0:T(128)S(1)} %fusion.208) | copy-start | bytes 1348
  12.5 282.7 %copy-start.19 = (f32[112]{0:T(128)}, f32[112]{0:T(128)S(1)}, u32[]{:S(2)}) copy-start(f32[112]{0:T(128)S(1)} %add_rsqrt_fusion) | copy-start | bytes 1348
  284.7 6.6 copy-start.5
  284.7 6.6 copy-start.15
  291.3 3.9 copy-start
  291.3 3.9 copy-start.3
  296.7 11.3 %copy-start.11 = (bf16[1,112,2048]{2,1,0:T(8,128)(2,1)S(1)}, bf16[1,112,2048]{2,1,0:T(8,128)(2,1)}, u32[]{:S(2)}) copy-start(bf16[1,112,2048]{2,1,0:T(8,128)(2,1)} %param.16) | copy-start | bytes 1376260
  298.6 18.3 %all-to-all-start = ((s32[16,1,112]{2,1,0:T(1,128)}), s32[16,1,112]{2,1,0:T(1,128)S(1)}, u32[]{:S(2)}, u32[]{:S(2)}) async-start(s32[16,1,112]{2,1,0:T(1,128)} %broadcast_in_dim.184), calls=%async_computation | async-start | bytes 16384 | tf_op jit(solution)/shard_map/all_to_all | solution.py:17
  308.0 295.1 %reduce-scatter.9.cloned.1.call-start = ((), (), s32[]{:S(2)}) async-start(), calls=%async_computation.9 | async-start | bytes 2064384 | tf_op jit(solution)/shard_map/reduce_scatter | solution.py:48
  314.3 12.3 %copy-start.7 = (bf16[4,112,4,128]{3,1,2,0:T(8,128)(2,1)}, bf16[4,112,4,128]{3,1,2,0:T(8,128)(2,1)S(1)}, u32[]{:S(2)}) copy-start(bf16[4,112,4,128]{3,1,2,0:T(8,128)(2,1)S(1)} %fusion.218) | copy-start | bytes 1376260
  472.2 3.6 copy-start.23
  476.0 2.6 copy-start.24
  483.1 3.6 copy-start.23
  486.8 2.6 copy-start.24
  493.9 3.5 copy-start.23
  497.6 2.6 copy-start.24
  504.7 3.6 copy-start.23
  564.3 81.5 %reduce-scatter.5.cloned.1.call-start = ((), (), s32[]{:S(2)}) async-start(), calls=%async_computation.7 | async-start | bytes 2064384 | tf_op jit(solution)/shard_map/reduce_scatter | solution.py:48
  565.5 103.1 %reduce-scatter.11.cloned.1.call-start = ((), (), s32[]{:S(2)}) async-start(), calls=%async_computation.10 | async-start | bytes 344064 | tf_op jit(solution)/shard_map/reduce_scatter | solution.py:48
  572.1 31.1 %copy-start.8 = (bf16[4,112,4,128]{3,1,2,0:T(8,128)(2,1)S(1)}, bf16[4,112,4,128]{3,1,2,0:T(8,128)(2,1)}, u32[]{:S(2)}) copy-start(bf16[4,112,4,128]{3,1,2,0:T(8,128)(2,1)} %copy-done.7) | copy-start | bytes 1376260
  572.1 31.1 %copy-start.10 = (bf16[4,1792,128]{2,1,0:T(8,128)(2,1)S(1)}, bf16[4,1792,128]{2,1,0:T(8,128)(2,1)}, u32[]{:S(2)}) copy-start(bf16[4,1792,128]{2,1,0:T(8,128)(2,1)} %get-tuple-element.1039) | copy-start | bytes 5505028
  603.2 83.8 %reduce-scatter.7.cloned.1.call-start = ((), (), s32[]{:S(2)}) async-start(), calls=%async_computation.8 | async-start | bytes 344064 | tf_op jit(solution)/shard_map/reduce_scatter | solution.py:48
  651.3 48.4 %collective-permute-start = (bf16[1,112,2048]{2,1,0:T(8,128)(2,1)}, bf16[1,112,2048]{2,1,0:T(8,128)(2,1)S(1)}, u32[]{:S(2)}, u32[]{:S(2)}) collective-permute-start(bf16[1,112,2048]{2,1,0:T(8,128)(2,1)} %fusion.165), channel_id=1, source_target_pairs={{240,0},{0,16},{16,32},{32,48},{48,64},{64,80},{80,96},{96,112},{1... | collective-permute-start | bytes 1376264 | tf_op jit(solution)/shard_map/ppermute | solution.py:43
  688.0 4.0 copy-start.6
  688.0 4.0 copy-start.13
  688.0 4.0 copy-start.14
  692.0 6.5 copy-start.22
  692.0 6.5 copy-start.12
  692.0 6.5 copy-start.18
  698.8 9.5 %collective-permute-start.1 = (bf16[1,112,2048]{2,1,0:T(8,128)(2,1)S(1)}, bf16[1,112,2048]{2,1,0:T(8,128)(2,1)S(1)}, u32[]{:S(2)}, u32[]{:S(2)}) collective-permute-start(bf16[1,112,2048]{2,1,0:T(8,128)(2,1)S(1)} %fusion.192), channel_id=1, source_target_pairs={{16,0},{32,16},{48,32},{64,48},{80,64},{96,80},{112,96},{128,112},... | collective-permute-start | bytes 1376264 | tf_op jit(solution)/shard_map/ppermute | solution.py:43
  (8 other events, 12.9 us)
Sparse Core Ops, SparseCore 0:
  9.8 270.2 all-gather.2
  298.1 163.5 all-gather.4
  564.4 38.6 reduce-scatter.8
  605.6 40.2 reduce-scatter.4
  648.2 20.3 reduce-scatter.10
  670.9 15.9 reduce-scatter.6
where the time goes:
time: 719 us; the launch traced here: 717 us
  waiting for transfers between devices  469 us (65%)
  matrix products  130 us (18%)
  local copies, waits for them, and re-layouts  60.4 us (8%)
  other arithmetic  24.8 us (3%)
  starting transfers between devices  18.2 us (3%)
  between operations  14.6 us (2%)
    all_gather x2, waiting for transfers between devices, side_by_side(): filled = lax.all_gather(both, axis, axis=dim, tiled=True)  382 us
    reduce_scatter x4, waiting for transfers between devices, summed_rows(): shard = lax.psum_scatter(shard, axis, scatter_dimension=dim, tiled=True)  77.6 us
    dot_general x16, matrix products, one_head(): jnp.einsum('grs,sd->rgd', rounded, value_block, preferred_element_type=jn...  40 us
    dot_general x8, matrix products, one_head(): jnp.einsum('rgd,sd->grs', query_block, key_block, preferred_element_type=...  27.6 us
    sub x8, matrix products, one_head(): numerators = jnp.where(visible, jnp.exp(masked - row_max), 0.0)  22.4 us
    dot_general x2, local copies, waits for them, and re-layouts, project(): jnp.dot(normed, query_matrix, preferred_element_type=jnp.float32)  20.7 us
    dot_general x3, matrix products, project(): jnp.dot(normed, query_matrix, preferred_element_type=jnp.float32)  18.9 us
  transfers between devices with their start and end apart: 9, of which 7 were waited for; matrix products, arithmetic and copies ran while one was open for 13% of the time, Pallas kernels for 0%

commit v1 on v0

v1 whole, which is shorter than its diff:
```python
import functools

import jax
import jax.numpy as jnp
from jax import lax
from jax.experimental import pallas as pl
from jax.experimental.pallas import tpu as pltpu
from jax.sharding import PartitionSpec as P

MESH = pl.DeviceIdType.MESH
F32 = jnp.float32
BF16 = jnp.bfloat16
HEAD_DIM = 128
LANES = 256
norm_eps = 1e-05
rope_base = 500000.0
LOG2E = 1.4426950408889634
HIDDEN = -1e30


def dot(a, b):
    return jnp.dot(a, b, preferred_element_type=F32)


def dot_nt(a, b):
    return lax.dot_general(a, b, (((1,), (1,)), ((), ())), preferred_element_type=F32)


def fold_rows(a, op):
    return op(a.reshape(a.shape[0] // 8, 8, a.shape[1]), axis=0)


def tick(
    planes,
    rows,
    xs_in,
    xf_in,
    dy_in,
    pos_in,
    tab_in,
    gain_in,
    wq_hbm,
    wkv_hbm,
    wo_hbm,
    next_out,
    grad_out,
    wbuf,
    wo,
    xbuf,
    tabs,
    posb,
    normed,
    acc,
    qnat,
    qt,
    kv,
    kvt,
    dkv,
    bias,
    qpos,
    dmt,
    score,
    prob,
    dsc,
    stage,
    landed,
    mix,
    mixed,
    dqkv,
    dnsend,
    dnrecv,
    dnown,
    loc_sem,
    x_send,
    x_recv,
    w_send,
    w_recv,
    pos_send,
    pos_recv,
    kv_send,
    kv_recv,
    rs_send,
    rs_recv,
):
    me = lax.axis_index("ctx")
    z = me // 2
    h = me % 2
    partner = z * 2 + 1 - h
    up = ((z + 1) % planes) * 2 + h
    down = ((z + planes - 1) % planes) * 2 + h
    width = wbuf.shape[2]
    half = width // 2
    pair = 2 * rows
    keys = planes * pair
    chunk = 256
    chunks = keys // chunk
    mine = pl.ds(pl.multiple_of(h * rows, 16), rows)
    theirs = pl.ds(pl.multiple_of((1 - h) * rows, 16), rows)
    to_z = (up, down)
    scale = HEAD_DIM ** (-0.5)

    barrier = pltpu.get_barrier_semaphore()
    for other in (partner, up, down):
        pl.semaphore_signal(barrier, inc=1, device_id={"ctx": other}, device_id_type=MESH)

    def local(src, dst, n):
        return pltpu.make_async_copy(src, dst, loc_sem.at[n])

    def remote(src, dst, s, r, to):
        return pltpu.make_async_remote_copy(
            src_ref=src, dst_ref=dst, send_sem=s, recv_sem=r, device_id={"ctx": to}, device_id_type=MESH
        )

    def to_partner(src, dst, n):
        return remote(src, dst, x_send.at[n], x_recv.at[n], partner)

    def pieces(side):
        out = []
        for j in range(2):
            g = 2 * side + j
            wide = pl.ds(pl.multiple_of(g * 512, 512), 512)
            key = pl.ds(pl.multiple_of(g * 128, 128), 128)
            value = pl.ds(pl.multiple_of(512 + g * 128, 128), 128)
            out.append((wq_hbm.at[:, wide], j, pl.ds(0, 512)))
            out.append((wkv_hbm.at[:, key], j, pl.ds(512, 128)))
            out.append((wkv_hbm.at[:, value], j, pl.ds(640, 128)))
        return out

    my_rows = pl.ds(pl.multiple_of(h * half, 128), half)
    own = [local(src, wbuf.at[j, z, my_rows, cols], n) for n, (src, j, cols) in enumerate(pieces(h))]
    for c in own:
        c.start()
    load_wo = local(wo_hbm, wo, 6)
    load_wo.start()
    keep_pos = local(pos_in, posb.at[me], 7)
    keep_pos.start()

    for n in range(3):
        xbuf[n, pl.ds(pair, LANES - pair), :] = jnp.zeros((LANES - pair, xbuf.shape[2]), BF16)
    for n in range(2):
        tabs[n, pl.ds(pair, LANES - pair), :] = jnp.zeros((LANES - pair, HEAD_DIM), F32)

    pl.semaphore_wait(barrier, 3)

    swap = [
        to_partner(pos_in, posb.at[me], 0),
        to_partner(tab_in, tabs.at[:, mine, :], 1),
    ]
    for n, (src, j, cols) in enumerate(pieces(1 - h)):
        swap.append(to_partner(src, wbuf.at[j, z, my_rows, cols], 2 + n))
    for n, src in enumerate((xs_in, xf_in, dy_in)):
        swap.append(to_partner(src, xbuf.at[n, mine, :], 8 + n))
    for c in swap:
        c.start()

    def w_copy(j, t, c):
        p = (z + planes - t) % planes if j == 0 else (z + t) % planes
        who = h if c == 0 else 1 - h
        block = wbuf.at[j, p, pl.ds(pl.multiple_of(who * half, 128), half), :]
        return remote(block, block, w_send.at[j, t, c], w_recv.at[j, t, c], to_z[j])

    def pos_copy(t):
        p = (z + planes - t) % planes
        block = posb.at[pl.ds(2 * p, 2)]
        return remote(block, block, pos_send.at[t], pos_recv.at[t], up)

    def w_step(t):
        for c in range(2):
            for j in range(2):
                if t > 0:
                    w_copy(j, t - 1, c).wait_recv()
                elif c == 0:
                    for n in range(3 * j, 3 * j + 3):
                        own[n].wait()
                else:
                    for n in range(3 * j, 3 * j + 3):
                        swap[2 + n].wait_recv()
                w_copy(j, t, c).start()
            if c == 0 and t == 0:
                for n, src in enumerate((xs_in, xf_in, dy_in)):
                    xbuf[n, mine, :] = src[...]
                tabs[:, mine, :] = tab_in[...]
            if c == 1:
                if t > 0:
                    pos_copy(t - 1).wait_recv()
                else:
                    keep_pos.wait()
                    swap[0].wait_recv()
                pos_copy(t).start()

    def norms():
        for n in range(2):
            def body(i, _):
                at = pl.ds(pl.multiple_of(i * 32, 32), 32)
                x = xbuf[n, at, :].astype(F32)
                inverse = lax.rsqrt(jnp.mean(x * x, axis=-1, keepdims=True) + norm_eps)
                y = (x * inverse * gain_in[...]).astype(BF16)
                for p in range(planes):
                    normed[p, pl.ds(pl.multiple_of(n * LANES + i * 32, 32), 32), :] = y[:, p * width : (p + 1) * width]
                return 0

            lax.fori_loop(0, LANES // 32, body, 0)

    def project(j, p, first):
        a = normed[p]
        if first:
            acc[j] = dot(a, wbuf[j, p])
        else:
            acc[j] += dot(a, wbuf[j, p])

    def grads_in():
        def body(n, _):
            at = pl.ds(pl.multiple_of(h * 1024 + n * 128, 128), 128)
            dmt[n] = dot_nt(wo[at, :], xbuf[2]).astype(BF16)
            return 0

        lax.fori_loop(0, 8, body, 0)

    for t in range(planes - 1):
        w_step(t)
        if t == 2:
            swap[1].wait_recv()
            swap[8].wait_recv()
            swap[9].wait_recv()
            norms()
            for j in range(2):
                project(j, z, True)
        if t == 3:
            for j in range(2):
                for s in (1, 2, 3):
                    p = (z + planes - s) % planes if j == 0 else (z + s) % planes
                    project(j, p, False)
        if t > 3:
            for j in range(2):
                p = (z + planes - t) % planes if j == 0 else (z + t) % planes
                project(j, p, False)
        if t == 4:
            load_wo.wait()
            swap[10].wait_recv()
            grads_in()
    t = planes - 1
    for c in range(2):
        for j in range(2):
            w_copy(j, t - 1, c).wait_recv()
    pos_copy(t - 1).wait_recv()
    for j in range(2):
        p = (z + planes - t) % planes if j == 0 else (z + t) % planes
        project(j, p, False)

    def rotated(x, sign):
        return x * tabs[0] + sign * (pltpu.roll(x, HEAD_DIM // 2, 1) * tabs[1])

    at_z = pl.ds(pl.multiple_of(z * pair, 32), pair)

    def make_kv(m):
        for j in range(2):
            a = acc.at[j, pl.ds(m * LANES, LANES), :]
            kv[m, j, 0, at_z, :] = rotated(a[:, 512:640], 1.0).astype(BF16)[:pair]
            kv[m, j, 1, at_z, :] = a[:, 640:768].astype(BF16)[:pair]

    def make_q(m):
        for j in range(2):
            a = acc.at[j, pl.ds(m * LANES, LANES), :]
            for r in range(4):
                q = rotated(a[:, r * 128 : r * 128 + 128], 1.0)
                if m == 0:
                    qnat[4 * j + r] = q.astype(BF16)
                qt[m, 4 * j + r] = q.T.astype(BF16)

    def kv_copy(m, j, k, t):
        p = (z + planes - t) % planes if j == 0 else (z + t) % planes
        block = kv.at[m, j, k, pl.ds(pl.multiple_of(p * pair, 32), pair), :]
        return remote(block, block, kv_send.at[m, j, k, t], kv_recv.at[m, j, k, t], to_z[j])

    def kv_start(m, t):
        for k in range(2):
            for j in range(2):
                kv_copy(m, j, k, t).start()

    def kv_step(m, t):
        for k in range(2):
            for j in range(2):
                kv_copy(m, j, k, t - 1).wait_recv()
                kv_copy(m, j, k, t).start()

    def make_bias():
        row0 = posb[2 * z][0:1, :]
        row1 = posb[2 * z + 1][0:1, :]
        zero = jnp.zeros_like(row0)
        wide0 = jnp.concatenate([row0, zero], axis=1)
        wide1 = pltpu.roll(jnp.concatenate([row1, zero], axis=1), rows, 1)
        lane = lax.broadcasted_iota(jnp.int32, (1, LANES), 1)
        query = jnp.where(lane < rows, wide0, jnp.where(lane < pair, wide1, 1e9))

        def body(i, _):
            column = jnp.broadcast_to(posb[i][0:1, :], (128, 128)).T
            column = jnp.concatenate([column, column], axis=1)[:rows]
            at = pl.ds(pl.multiple_of(i * rows, 16), rows)
            bias[at, :] = jnp.where(column <= query, 0.0, HIDDEN)
            return 0

        lax.fori_loop(0, 2 * planes, body, 0)

    def transposed(m):
        for j in range(2):
            for k in range(2):
                def body(i, _):
                    at = pl.ds(pl.multiple_of(i * 128, 128), 128)
                    kvt[j, k, :, at] = kv[m, j, k, at, :].astype(F32).T.astype(BF16)
                    return 0

                lax.fori_loop(0, keys // 128, body, 0)

    def softmax(m, j, i):
        q = qt[m, i]
        top = jnp.full((8, LANES), HIDDEN, F32)
        for c in range(chunks):
            at = pl.ds(c * chunk, chunk)
            s = dot(kv[m, j, 0, at, :], q) + bias[at, :]
            score[at, :] = s
            top = jnp.maximum(top, fold_rows(s, jnp.max))
        top = jnp.max(top, axis=0, keepdims=True)
        total = jnp.zeros((8, LANES), F32)
        for c in range(chunks):
            at = pl.ds(c * chunk, chunk)
            e = jnp.exp2((score[at, :] - top) * (scale * LOG2E))
            total += fold_rows(e, jnp.sum)
            if m == 0:
                score[at, :] = e
            prob[at, :] = e.astype(BF16)
        return jnp.sum(total, axis=0, keepdims=True)

    def backward(i):
        j = i // 4
        inverse = 1.0 / softmax(0, j, i)
        summed = dot(kvt[j, 1], prob[...])
        dm = dmt[i].astype(F32)
        share = -jnp.sum(dm * summed, axis=0, keepdims=True) * (inverse * inverse)
        dsum = dm * inverse
        dsum_t = dsum.astype(BF16)
        dsum_n = dsum.T.astype(BF16)
        q = qnat[i]
        for c in range(chunks):
            at = pl.ds(c * chunk, chunk)
            dkv[j, 1, at, :] += dot(prob[at, :], dsum_n)
            ds = (score[at, :] * (dot(kv[0, j, 1, at, :], dsum_t) + share)).astype(BF16)
            dsc[at, :] = ds
            dkv[j, 0, at, :] += dot(ds, q) * scale
        dq = dot(kvt[j, 0], dsc[...]) * scale
        qnat[i] = dq.T.astype(BF16)

    def forward(i):
        j = i // 4
        inverse = 1.0 / softmax(1, j, i)
        mix[i] = (dot(kvt[j, 1], prob[...]) * inverse).T.astype(BF16)

    make_kv(0)
    kv_start(0, 0)
    make_q(0)
    make_kv(1)
    make_q(1)
    kv_step(0, 1)
    make_bias()
    for t in range(2, planes - 1):
        kv_step(0, t)
    kv_start(1, 0)
    for n in range(2):
        for k in range(2):
            dkv[n, k] = jnp.zeros((keys, HEAD_DIM), F32)
    for k in range(2):
        for j in range(2):
            kv_copy(0, j, k, planes - 2).wait_recv()
    transposed(0)

    def backward_step(i, _):
        backward(i)

        @pl.when(i < planes - 2)
        def _():
            kv_step(1, i + 1)

        return 0

    lax.fori_loop(0, 8, backward_step, 0)
    for k in range(2):
        for j in range(2):
            kv_copy(1, j, k, planes - 2).wait_recv()
    transposed(1)

    def rs_copy(j, k, t):
        return remote(stage.at[j, k, t], landed.at[j, k, t], rs_send.at[j, k, t], rs_recv.at[j, k, t], to_z[j])

    def rs_step(t, first):
        for k in range(2):
            for j in range(2):
                p = (z + 2 * planes - 1 - t) % planes if j == 0 else (z + 1 + t) % planes
                part = dkv[j, k, pl.ds(pl.multiple_of(p * pair, 32), pair), :]
                if not first:
                    rs_copy(j, k, t - 1).wait_recv()
                    part = part + landed[j, k, t - 1].astype(F32)
                stage[j, k, t] = part.astype(BF16)
                rs_copy(j, k, t).start()

    rs_step(0, True)

    def forward_step(i, _):
        forward(i)

        @pl.when(i < planes - 2)
        def _():
            rs_step(i + 1, False)

        return 0

    lax.fori_loop(0, 8, forward_step, 0)

    mix_swap = to_partner(mix.at[:, theirs, :], mixed.at[pl.ds(8 * h, 8)], 11)
    mix_swap.start()
    for n in range(8):
        mixed[8 * h + n] = mix[n, mine, :]

    def dq_body(i, _):
        d = qnat[i].astype(F32)
        dqkv[i] = (rotated(d, -1.0)).astype(BF16)
        return 0

    lax.fori_loop(0, 8, dq_body, 0)
    dq_all = [jnp.concatenate([dqkv[4 * j + r] for r in range(4)], axis=1) for j in range(2)]

    def dn_q(p, _):
        normed_grad = dot_nt(dq_all[0], wbuf[0, p, :, 0:512]) + dot_nt(dq_all[1], wbuf[1, p, :, 0:512])
        dnown[p] = normed_grad
        return 0

    lax.fori_loop(0, planes, dn_q, 0)

    mix_swap.wait_recv()
    heads_all = jnp.concatenate([mixed[n] for n in range(16)], axis=1)
    for n in range(planes):
        at = pl.ds(n * width, width)
        next_out[:, at] = (xf_in[:, at].astype(F32) + dot(heads_all, wo[:, at])).astype(BF16)

    t = planes - 1
    dkvs = []
    for j in range(2):
        for k in range(2):
            rs_copy(j, k, t - 1).wait_recv()
            part = dkv[j, k, at_z, :] + landed[j, k, t - 1].astype(F32)
            part = part.astype(BF16).astype(F32)
            part = jnp.concatenate([part, jnp.zeros((LANES - pair, HEAD_DIM), F32)], axis=0)
            if k == 0:
                part = rotated(part, -1.0)
            dkvs.append(part.astype(BF16))
    dkv_all = [jnp.concatenate(dkvs[2 * j : 2 * j + 2], axis=1) for j in range(2)]

    def dn_copy(p):
        return remote(dnsend.at[p], dnrecv.at[p], x_send.at[12 + p], x_recv.at[12 + p], partner)

    def dn_kv(p, _):
        dnown[p] += dot_nt(dkv_all[0], wbuf[0, p, :, 512:768]) + dot_nt(dkv_all[1], wbuf[1, p, :, 512:768])
        dnsend[p] = dnown[p, theirs, :].astype(BF16)
        dn_copy(p).start()
        return 0

    lax.fori_loop(0, planes, dn_kv, 0)
    x = xs_in[...].astype(F32)
    inverse = lax.rsqrt(jnp.mean(x * x, axis=-1, keepdims=True) + norm_eps)
    along = jnp.zeros((rows, 1), F32)
    for p in range(planes):
        dn_copy(p).wait_recv()
        at = slice(p * width, (p + 1) * width)
        d = (dnown[p, mine, :] + dnrecv[p].astype(F32)).astype(BF16).astype(F32) * gain_in[:, at]
        dnown[p, mine, :] = d
        along += jnp.sum(d * x[:, at], axis=-1, keepdims=True)
    pull = along * (1.0 / x.shape[1]) * (inverse * inverse * inverse)
    for p in range(planes):
        at = slice(p * width, (p + 1) * width)
        grad = (dnown[p, mine, :] * inverse - x[:, at] * pull).astype(BF16)
        grad_out[:, at] = grad + dy_in[:, at]

    for c in swap:
        c.wait_send()
    mix_swap.wait_send()
    for t in range(planes - 1):
        pos_copy(t).wait_send()
        for j in range(2):
            for c in range(2):
                w_copy(j, t, c).wait_send()
                rs_copy(j, c, t).wait_send()
                for m in range(2):
                    kv_copy(m, j, c, t).wait_send()
    for p in range(planes):
        dn_copy(p).wait_send()


def from_behind(block, axis, distance):
    devices = lax.axis_size(axis)
    route = [((i - distance) % devices, i) for i in range(devices)]
    return lax.ppermute(block, axis, route)


def shards(planes, xf, xs, dy, positions, gain, wq, wkv, wo):
    rows, features = xf.shape[1:]
    keys = 2 * planes * rows
    width = features // planes
    frequency = rope_base ** (-2.0 * jnp.arange(HEAD_DIM // 2, dtype=F32) / HEAD_DIM)
    where = positions.astype(F32)
    angles = where[:, None] * frequency[None, :]
    cos_table, sin_table = jnp.cos(angles), jnp.sin(angles)
    tables = jnp.stack(
        [
            jnp.concatenate([cos_table, cos_table], axis=1),
            jnp.concatenate([-sin_table, sin_table], axis=1),
        ]
    )
    pos_tile = jnp.broadcast_to(jnp.pad(where, (0, 128 - rows))[None, :], (8, 128))
    vmem = pl.BlockSpec(memory_space=pltpu.VMEM)
    hbm = pl.BlockSpec(memory_space=pl.ANY)
    hops = planes - 1
    dma = pltpu.SemaphoreType.DMA
    out = jax.ShapeDtypeStruct((rows, features), BF16)
    produced, grads = pl.pallas_call(
        functools.partial(tick, planes, rows),
        out_shape=(out, out),
        in_specs=[vmem] * 6 + [hbm] * 3,
        out_specs=(vmem, vmem),
        scratch_shapes=[
            pltpu.VMEM((2, planes, width, 768), BF16),
            pltpu.VMEM((features, features), BF16),
            pltpu.VMEM((3, LANES, features), BF16),
            pltpu.VMEM((2, LANES, HEAD_DIM), F32),
            pltpu.VMEM((2 * planes, 8, 128), F32),
            pltpu.VMEM((planes, 2 * LANES, width), BF16),
            pltpu.VMEM((2, 2 * LANES, 768), F32),
            pltpu.VMEM((8, LANES, HEAD_DIM), BF16),
            pltpu.VMEM((2, 8, HEAD_DIM, LANES), BF16),
            pltpu.VMEM((2, 2, 2, keys, HEAD_DIM), BF16),
            pltpu.VMEM((2, 2, HEAD_DIM, keys), BF16),
            pltpu.VMEM((2, 2, keys, HEAD_DIM), F32),
            pltpu.VMEM((keys, LANES), F32),
            pltpu.VMEM((1, LANES), F32),
            pltpu.VMEM((8, HEAD_DIM, LANES), BF16),
            pltpu.VMEM((keys, LANES), F32),
            pltpu.VMEM((keys, LANES), BF16),
            pltpu.VMEM((keys, LANES), BF16),
            pltpu.VMEM((2, 2, hops, 2 * rows, HEAD_DIM), BF16),
            pltpu.VMEM((2, 2, hops, 2 * rows, HEAD_DIM), BF16),
            pltpu.VMEM((8, LANES, HEAD_DIM), BF16),
            pltpu.VMEM((16, rows, HEAD_DIM), BF16),
            pltpu.VMEM((8, LANES, HEAD_DIM), BF16),
            pltpu.VMEM((planes, rows, width), BF16),
            pltpu.VMEM((planes, rows, width), BF16),
            pltpu.VMEM((planes, LANES, width), F32),
            dma((8,)),
            dma((12 + planes,)),
            dma((12 + planes,)),
            dma((2, hops, 2)),
            dma((2, hops, 2)),
            dma((hops,)),
            dma((hops,)),
            dma((2, 2, 2, hops)),
            dma((2, 2, 2, hops)),
            dma((2, 2, hops)),
            dma((2, 2, hops)),
        ],
        compiler_params=pltpu.CompilerParams(
            collective_id=0, has_side_effects=True, vmem_limit_bytes=67_043_328
        ),
        name="tick",
    )(xs[0], xf[0], dy[0], pos_tile, tables, gain, wq[0], wkv[0], wo[0])
    sent_on = from_behind(produced[None], "section", 1)
    sent_back = from_behind(grads[None], "section", -1)
    return sent_on, sent_back


def solution(mesh):
    placed = (
        P("section", "ctx", None),
        P("section", "ctx", None),
        P("section", "ctx", None),
        P("ctx"),
        P("section", None),
        P("section", "ctx", None),
        P("section", "ctx", None),
        P("section", None, None),
    )
    return jax.shard_map(
        functools.partial(shards, mesh.shape["ctx"] // 2),
        mesh=mesh,
        in_specs=placed,
        out_specs=(P("section", "ctx", None), P("section", "ctx", None)),
        check_vma=False,
    )
```

time: 719 us -> 209 us (0.29)
  waiting for transfers between devices: 469 us -> 10.3 us
  Pallas kernels: 0 us -> 175 us
  matrix products: 130 us -> 0 us
  local copies, waits for them, and re-layouts: 60.4 us -> 2.13 us
  other arithmetic: 24.8 us -> 1.7 us
  between operations: 14.6 us -> 0.66 us
    all_gather x2 -> x0, waiting for transfers between devices: 382 us -> none  [side_by_side(): filled = lax.all_gather(both, axis, axis=dim, tiled=True)]
    pallas_call x0 -> x1, Pallas kernels: none -> 175 us  [shards(): pl.pallas_call(functools.partial(tick, planes, rows), out_shape=(out, out...]
    dot_general x32 -> x0, matrix products: 107 us -> none  [the longest x16 40 us: one_head(): jnp.einsum('grs,sd->rgd', rounded, value_block, preferred_element_type=jn...]
    reduce_scatter x4 -> x0, waiting for transfers between devices: 77.6 us -> none  [summed_rows(): shard = lax.psum_scatter(shard, axis, scatter_dimension=dim, tiled=True)]
    dot_general x4 -> x0, local copies, waits for them, and re-layouts: 32 us -> none  [the longest x2 20.7 us: project(): jnp.dot(normed, query_matrix, preferred_element_type=jnp.float32)]
    sub x8 -> x0, matrix products: 22.4 us -> none  [one_head(): numerators = jnp.where(visible, jnp.exp(masked - row_max), 0.0)]
    while x16 -> x0, local copies, waits for them, and re-layouts: 10.6 us -> none
    ppermute x2, starting transfers between devices: 8.31 us -> 18.4 us  [from_behind(): return lax.ppermute(block, axis, route)]
  transfers between devices with their start and end apart: 9 -> 2, of which waited for: 7 -> 1; matrix products, arithmetic and copies ran while one was open for 13% -> 0% of each run, Pallas kernels for 0% -> 0%
where the time goes in v1:
time: 209 us; the launch traced here: 208 us
  Pallas kernels  175 us (84%)
  starting transfers between devices  18.4 us (9%)
  waiting for transfers between devices  10.3 us (5%)
  local copies, waits for them, and re-layouts  2.13 us (1%)
    pallas_call x1, Pallas kernels, shards(): pl.pallas_call(functools.partial(tick, planes, rows), out_shape=(out, out...  175 us
    ppermute x2, starting transfers between devices, from_behind(): return lax.ppermute(block, axis, route)  18.4 us
    ppermute x2, waiting for transfers between devices, from_behind(): return lax.ppermute(block, axis, route)  10.3 us
  transfers between devices with their start and end apart: 2, of which 1 were waited for; matrix products, arithmetic and copies ran while one was open for 0% of the time, Pallas kernels for 0%

profile of v1, /device:TPU:1, one launch (start us, length us, event | category | flops | bytes accessed | tf_op | source)
XLA Modules:
  0.0 207.8 jit_solution(2885917136880959346)
XLA Ops:
  0.6 0.7 convert_element_type.5
  1.3 0.3 multiply_cosine_fusion
  1.6 0.1 maximum_bitcast_fusion
  1.7 0.7 pad_maximum_fusion.tab_in
  2.4 0.6 broadcast_in_dim.6.pos_in
  2.9 174.6 %tick.1 = (bf16[112,2048]{1,0:T(8,128)(2,1)}, bf16[112,2048]{1,0:T(8,128)(2,1)}) custom-call(bf16[112,2048]{1,0:T(8,128)(2,1)} %bitcast.14, bf16[112,2048]{1,0:T(8,128)(2,1)} %bitcast.15, bf16[112,2048]{1,0:T(8,128)(2,1)} %bitcast.16, f32[8,128]{1,0:T(8,128)} %broadcast_in_dim.6.pos_in, f32[2,112,128]{2,1,0:T(8,128)} %pad_maximum_fusion.tab_in, ...), custom_call_target="tpu_custom_call" | custom-call | tf_op jit(solution)/shard_map/tick/pallas_call | solution.py:522
  177.6 16.0 %collective-permute-start.1 = (bf16[1,112,2048]{2,1,0:T(8,128)(2,1)}, bf16[1,112,2048]{2,1,0:T(8,128)(2,1)S(1)}, u32[]{:S(2)}, u32[]{:S(2)}) collective-permute-start(bf16[1,112,2048]{2,1,0:T(8,128)(2,1)} %bitcast.19), channel_id=1, source_target_pairs={{16,0},{32,16},{48,32},{64,48},{80,64},{96,80},{112,96},{128,112},... | collective-permute-start | bytes 1376264 | tf_op jit(solution)/shard_map/ppermute | solution.py:499
  193.5 2.5 %collective-permute-start = (bf16[1,112,2048]{2,1,0:T(8,128)(2,1)}, bf16[1,112,2048]{2,1,0:T(8,128)(2,1)S(1)}, u32[]{:S(2)}, u32[]{:S(2)}) collective-permute-start(bf16[1,112,2048]{2,1,0:T(8,128)(2,1)} %bitcast.18), channel_id=1, source_target_pairs={{240,0},{0,16},{16,32},{32,48},{48,64},{64,80},{80,96},{96,112},{1... | collective-permute-start | bytes 1376264 | tf_op jit(solution)/shard_map/ppermute | solution.py:499
  196.0 10.3 %collective-permute-done.1 = bf16[1,112,2048]{2,1,0:T(8,128)(2,1)S(1)} collective-permute-done((bf16[1,112,2048]{2,1,0:T(8,128)(2,1)}, bf16[1,112,2048]{2,1,0:T(8,128)(2,1)S(1)}, u32[]{:S(2)}, u32[]{:S(2)}) %collective-permute-start.1) | collective-permute-done | bytes 458784 | tf_op jit(solution)/shard_map/ppermute | solution.py:499
  206.3 0.0 collective-permute-done
  206.3 0.8 copy.12
  207.0 0.8 copy.13
  (2 shorter events, 0.0 us)
Async XLA Ops:
  177.6 28.7 %collective-permute-start.1 = (bf16[1,112,2048]{2,1,0:T(8,128)(2,1)}, bf16[1,112,2048]{2,1,0:T(8,128)(2,1)S(1)}, u32[]{:S(2)}, u32[]{:S(2)}) collective-permute-start(bf16[1,112,2048]{2,1,0:T(8,128)(2,1)} %bitcast.19), channel_id=1, source_target_pairs={{16,0},{32,16},{48,32},{64,48},{80,64},{96,80},{112,96},{128,112},... | collective-permute-start | bytes 1376264 | tf_op jit(solution)/shard_map/ppermute | solution.py:499
  193.5 12.8 %collective-permute-start = (bf16[1,112,2048]{2,1,0:T(8,128)(2,1)}, bf16[1,112,2048]{2,1,0:T(8,128)(2,1)S(1)}, u32[]{:S(2)}, u32[]{:S(2)}) collective-permute-start(bf16[1,112,2048]{2,1,0:T(8,128)(2,1)} %bitcast.18), channel_id=1, source_target_pairs={{240,0},{0,16},{16,32},{32,48},{48,64},{64,80},{80,96},{96,112},{1... | collective-permute-start | bytes 1376264 | tf_op jit(solution)/shard_map/ppermute | solution.py:499

commit v2 on v1

v2 whole, which is shorter than its diff:
```python
import functools

import jax
import jax.numpy as jnp
from jax import lax
from jax.experimental import pallas as pl
from jax.experimental.pallas import tpu as pltpu
from jax.sharding import PartitionSpec as P

MESH = pl.DeviceIdType.MESH
F32 = jnp.float32
BF16 = jnp.bfloat16
HEAD_DIM = 128
LANES = 256
norm_eps = 1e-05
rope_base = 500000.0
LOG2E = 1.4426950408889634
HIDDEN = -1e30


def dot(a, b):
    return jnp.dot(a, b, preferred_element_type=F32)


def dot_nt(a, b):
    return lax.dot_general(a, b, (((1,), (1,)), ((), ())), preferred_element_type=F32)


def fold_rows(a, op):
    return op(a.reshape(a.shape[0] // 8, 8, a.shape[1]), axis=0)


def tick(
    planes,
    rows,
    xs_in,
    xf_in,
    dy_in,
    pos_in,
    tab_in,
    gain_in,
    wq_hbm,
    wkv_hbm,
    wo_hbm,
    next_out,
    grad_out,
    wkvb,
    wqb,
    wo,
    xbuf,
    tabs,
    posb,
    normed,
    acc_kv,
    acc_q,
    qnat,
    qt,
    kv,
    kvt,
    dkv,
    bias,
    dmt,
    score,
    prob,
    dsc,
    stage,
    landed,
    mix,
    mixed,
    dnsend,
    dnrecv,
    dnown,
    fout,
    gout,
    loc_sem,
    x_send,
    x_recv,
    ring_send,
    ring_recv,
    rs_send,
    rs_recv,
    out_send,
    out_recv,
):
    me = lax.axis_index("ctx")
    section = lax.axis_index("section")
    sections = lax.axis_size("section")
    z = me // 2
    h = me % 2
    partner = z * 2 + 1 - h
    to_z = (((z + 1) % planes) * 2 + h, ((z + planes - 1) % planes) * 2 + h)
    following = (section + 1) % sections
    preceding = (section + sections - 1) % sections
    width = wkvb.shape[1]
    half = width // 2
    pair = 2 * rows
    keys = planes * pair
    chunk = 256
    chunks = keys // chunk
    far = planes // 2
    mine = pl.ds(pl.multiple_of(h * rows, 16), rows)
    theirs = pl.ds(pl.multiple_of((1 - h) * rows, 16), rows)
    scale = HEAD_DIM ** (-0.5)
    scope = jax.named_scope

    barrier = pltpu.get_barrier_semaphore()
    for other in (partner, *to_z):
        pl.semaphore_signal(barrier, inc=1, device_id={"ctx": other}, device_id_type=MESH)
    for other in (following, preceding):
        pl.semaphore_signal(barrier, inc=1, device_id={"section": other}, device_id_type=MESH)

    def local(src, dst, n):
        return pltpu.make_async_copy(src, dst, loc_sem.at[n])

    def remote(src, dst, s, r, **to):
        return pltpu.make_async_remote_copy(
            src_ref=src, dst_ref=dst, send_sem=s, recv_sem=r, device_id=to, device_id_type=MESH
        )

    def to_partner(src, dst, n):
        return remote(src, dst, x_send.at[n], x_recv.at[n], ctx=partner)

    def plane(offset):
        return (z + 2 * planes + offset) % planes

    def pieces(side):
        pairs = []
        for n in range(2):
            at = pl.ds(pl.multiple_of(512 * n + side * 256, 256), 256)
            pairs.append((wkv_hbm.at[:, at], wkvb.at[z, my_rows, pl.ds(256 * n, 256)]))
        for j in range(2):
            at = pl.ds(pl.multiple_of(side * 1024 + j * 512, 512), 512)
            pairs.append((wq_hbm.at[:, at], wqb.at[j, z, my_rows, :]))
        return pairs

    my_rows = pl.ds(pl.multiple_of(h * half, 128), half)
    own = [local(src, dst, n) for n, (src, dst) in enumerate(pieces(h))]
    keep_pos = local(pos_in, posb.at[me], 5)
    for c in (*own, keep_pos):
        c.start()
    load_wo = local(wo_hbm, wo, 4)
    load_wo.start()

    with scope("barrier"):
        pl.semaphore_wait(barrier, 5)

    given = pieces(1 - h)
    tokens = [(src, xbuf.at[n, mine, :]) for n, src in enumerate((xs_in, xf_in, dy_in))]
    swaps = [
        *given[:2],
        (pos_in, posb.at[me]),
        (tab_in, tabs.at[:, mine, :]),
        tokens[0],
        *given[2:],
        *tokens[1:],
    ]
    swap = [to_partner(src, dst, n) for n, (src, dst) in enumerate(swaps)]
    for c in swap:
        c.start()

    class Ring:
        def __init__(self, number, parts):
            self.number, self.parts = number, parts

        def copy(self, n, way, t):
            block = self.parts[n][0](plane(-t if way == 0 else t))
            sems = (self.number, n, way, t)
            return remote(block, block, ring_send.at[sems], ring_recv.at[sems], ctx=to_z[way])

        def step(self, t, ready=None):
            for n, (_, *hops) in enumerate(self.parts):
                if t == 0 and ready is not None:
                    ready(n)
                for way in range(2):
                    if 0 < t <= hops[way]:
                        self.copy(n, way, t - 1).wait_recv()
                    if t < hops[way]:
                        self.copy(n, way, t).start()

        def sent(self):
            for n, (_, *hops) in enumerate(self.parts):
                for way in range(2):
                    for t in range(hops[way]):
                        self.copy(n, way, t).wait_send()

    def rows_of(ref, c):
        who = h if c == 0 else 1 - h
        at = pl.ds(pl.multiple_of(who * half, 128), half)
        return lambda p: ref.at[p, at, :]

    def w_parts(ref):
        return [(rows_of(ref, 0), far, far - 1), (rows_of(ref, 1), far - 1, far)]

    def kv_parts(m):
        def block(j):
            return lambda p: kv.at[m, j, :, pl.ds(pl.multiple_of(p * pair, 32), pair), :]

        return [(block(0), far, far - 1), (block(1), far - 1, far)]

    pos_part = (lambda p: posb.at[pl.ds(2 * p, 2)], far, far - 1)
    ring_wkv = Ring(0, [*w_parts(wkvb), pos_part])
    ring_q = [Ring(1 + j, w_parts(wqb.at[j])) for j in range(2)]
    ring_kv = [Ring(3 + m, kv_parts(m)) for m in range(2)]

    def ready_wkv(n):
        if n == 0:
            own[0].wait()
            own[1].wait()
        elif n == 1:
            swap[0].wait_recv()
            swap[1].wait_recv()
        else:
            keep_pos.wait()
            swap[2].wait_recv()

    def ready_q(j):
        def ready(n):
            if n == 0:
                own[2 + j].wait()
            else:
                swap[5 + j].wait_recv()

        return ready

    def norms(n):
        def body(i, _):
            at = pl.ds(pl.multiple_of(i * 32, 32), 32)
            x = xbuf[n, at, :].astype(F32)
            inverse = lax.rsqrt(jnp.mean(x * x, axis=-1, keepdims=True) + norm_eps)
            y = (x * inverse * gain_in[...]).astype(BF16)
            for p in range(planes):
                normed[p, pl.ds(pl.multiple_of(n * LANES + i * 32, 32), 32), :] = y[:, p * width : (p + 1) * width]
            return 0

        lax.fori_loop(0, LANES // 32, body, 0)

    def project_kv(m):
        at = pl.ds(m * LANES, LANES)
        total = dot(normed[0, at, :], wkvb[0])
        for p in range(1, planes):
            total += dot(normed[p, at, :], wkvb[p])
        acc_kv[...] = total

    def project_q(j, offsets, first=False):
        ps = [plane(o) for o in offsets]
        total = dot(normed[ps[0]], wqb[j, ps[0]])
        for p in ps[1:]:
            total += dot(normed[p], wqb[j, p])
        if first:
            acc_q[j] = total
        else:
            acc_q[j] += total

    def grads_in():
        def body(n, _):
            at = pl.ds(pl.multiple_of(h * 1024 + n * 128, 128), 128)
            dmt[n] = dot_nt(wo[at, :], xbuf[2]).astype(BF16)
            return 0

        lax.fori_loop(0, 8, body, 0)

    def rotated(x, sign):
        return x * tabs[0] + sign * (pltpu.roll(x, HEAD_DIM // 2, 1) * tabs[1])

    at_z = pl.ds(pl.multiple_of(z * pair, 32), pair)

    def make_kv(m):
        for j in range(2):
            key = acc_kv[:, 128 * j : 128 * j + 128]
            kv[m, j, 0, at_z, :] = rotated(key, 1.0).astype(BF16)[:pair]
            kv[m, j, 1, at_z, :] = acc_kv[:, 256 + 128 * j : 384 + 128 * j].astype(BF16)[:pair]

    def make_q(j, m):
        for r in range(4):
            q = rotated(acc_q[j, m * LANES : (m + 1) * LANES, r * 128 : r * 128 + 128], 1.0)
            if m == 0:
                qnat[4 * j + r] = q.astype(BF16)
            qt[m, 4 * j + r] = q.T.astype(BF16)

    def make_bias():
        row0 = posb[2 * z][0:1, :]
        row1 = posb[2 * z + 1][0:1, :]
        zero = jnp.zeros_like(row0)
        wide0 = jnp.concatenate([row0, zero], axis=1)
        wide1 = pltpu.roll(jnp.concatenate([row1, zero], axis=1), rows, 1)
        lane = lax.broadcasted_iota(jnp.int32, (1, LANES), 1)
        query = jnp.where(lane < rows, wide0, jnp.where(lane < pair, wide1, 1e9))

        def body(i, _):
            column = jnp.broadcast_to(posb[i][0:1, :], (128, 128)).T
            column = jnp.concatenate([column, column], axis=1)[:rows]
            at = pl.ds(pl.multiple_of(i * rows, 16), rows)
            bias[at, :] = jnp.where(column <= query, 0.0, HIDDEN)
            return 0

        lax.fori_loop(0, 2 * planes, body, 0)

    def transposed(m, ks):
        for j in range(2):
            for k in ks:
                for i in range(keys // 128):
                    at = pl.ds(i * 128, 128)
                    kvt[j, k, :, at] = kv[m, j, k, at, :].astype(F32).T.astype(BF16)

    def softmax(m, j, i):
        q = qt[m, i]
        top = jnp.full((8, LANES), HIDDEN, F32)
        for c in range(chunks):
            at = pl.ds(c * chunk, chunk)
            s = dot(kv[m, j, 0, at, :], q) + bias[at, :]
            score[at, :] = s
            top = jnp.maximum(top, fold_rows(s, jnp.max))
        top = jnp.max(top, axis=0, keepdims=True)
        total = jnp.zeros((8, LANES), F32)
        for c in range(chunks):
            at = pl.ds(c * chunk, chunk)
            e = jnp.exp2((score[at, :] - top) * (scale * LOG2E))
            total += fold_rows(e, jnp.sum)
            if m == 0:
                score[at, :] = e
            prob[at, :] = e.astype(BF16)
        return jnp.sum(total, axis=0, keepdims=True)

    def backward(j, i):
        inverse = 1.0 / softmax(0, j, i)
        summed = dot(kvt[j, 1], prob[...])
        dm = dmt[i].astype(F32)
        share = -jnp.sum(dm * summed, axis=0, keepdims=True) * (inverse * inverse)
        dsum = dm * inverse
        dsum_t = dsum.astype(BF16)
        dsum_n = dsum.T.astype(BF16)
        q = qnat[i]
        for c in range(chunks):
            at = pl.ds(c * chunk, chunk)
            dkv[j, 1, at, :] += dot(prob[at, :], dsum_n)
            ds = (score[at, :] * (dot(kv[0, j, 1, at, :], dsum_t) + share)).astype(BF16)
            dsc[at, :] = ds
            dkv[j, 0, at, :] += dot(ds, q) * scale
        dq = dot(kvt[j, 0], dsc[...]) * scale
        qnat[i] = dq.T.astype(BF16)

    def forward(j, i):
        inverse = 1.0 / softmax(1, j, i)
        mix[i] = (dot(kvt[j, 1], prob[...]) * inverse).T.astype(BF16)

    rs_hops = ((far - 1, far), (far, far - 1))

    def rs_copy(j, k, way, t):
        at = (j, k, way, t)
        return remote(stage.at[at], landed.at[at], rs_send.at[at], rs_recv.at[at], ctx=to_z[way])

    def rs_step(j, t):
        for k in range(2):
            for way in range(2):
                hops = rs_hops[k][way]
                if 0 < t <= hops:
                    rs_copy(j, k, way, t - 1).wait_recv()
                if t < hops:
                    p = plane(hops - t if way == 0 else t - hops)
                    part = dkv[j, k, pl.ds(pl.multiple_of(p * pair, 32), pair), :]
                    if t > 0:
                        part = part + landed[j, k, way, t - 1].astype(F32)
                    stage[j, k, way, t] = part.astype(BF16)
                    rs_copy(j, k, way, t).start()

    def in_order(i, **steps):
        for name, work in steps.items():
            pl.when(i == int(name[1:]))(work)

    for n in range(3):
        xbuf[n, pl.ds(pair, LANES - pair), :] = jnp.zeros((LANES - pair, xbuf.shape[2]), BF16)
    for n in range(2):
        tabs[n, pl.ds(pair, LANES - pair), :] = jnp.zeros((LANES - pair, HEAD_DIM), F32)
    for n, src in enumerate((xs_in, xf_in, dy_in)):
        xbuf[n, mine, :] = src[...]
    tabs[:, mine, :] = tab_in[...]
    for n in range(2):
        for k in range(2):
            dkv[n, k] = jnp.zeros((keys, HEAD_DIM), F32)

    with scope("a0"):
        ring_wkv.step(0, ready_wkv)
    with scope("a1"):
        ring_wkv.step(1)
    with scope("a2"):
        ring_wkv.step(2)
    with scope("a3"):
        ring_wkv.step(3)
    with scope("c0"):
        ring_q[0].step(0, ready_q(0))
    with scope("norms0"):
        swap[3].wait_recv()
        swap[4].wait_recv()
        norms(0)
    with scope("a4"):
        ring_wkv.step(4)
    with scope("kv0"):
        project_kv(0)
        make_kv(0)
    ring_kv[0].step(0)
    with scope("norms1"):
        swap[7].wait_recv()
        norms(1)
    with scope("c1"):
        ring_q[0].step(1)
    with scope("q0a"):
        project_q(0, (0, 1, -1), True)
    with scope("b1"):
        ring_kv[0].step(1)
    with scope("bias"):
        make_bias()
    with scope("c2"):
        ring_q[0].step(2)
    with scope("q0b"):
        project_q(0, (2, -2))
    with scope("b2"):
        ring_kv[0].step(2)
    with scope("kv1"):
        project_kv(1)
        make_kv(1)
    with scope("c3"):
        ring_q[0].step(3)
    with scope("q0c"):
        project_q(0, (3, -3))
    with scope("b3"):
        ring_kv[0].step(3)
    ring_q[1].step(0, ready_q(1))
    with scope("dm"):
        load_wo.wait()
        swap[8].wait_recv()
        grads_in()
    with scope("c4"):
        ring_q[0].step(4)
    with scope("q0d"):
        project_q(0, (4,))
        make_q(0, 0)
    with scope("b4"):
        ring_kv[0].step(4)
    with scope("t0"):
        transposed(0, (0, 1))
    with scope("d1"):
        ring_q[1].step(1)

    def backward0(i, _):
        with scope("bwd"):
            backward(0, i)

        def first():
            with scope("d2"):
                ring_q[1].step(2)

        def second():
            with scope("d3"):
                ring_q[1].step(3)
            ring_kv[1].step(0)

        in_order(i, i1=first, i3=second)
        return 0

    lax.fori_loop(0, 4, backward0, 0)
    rs_step(0, 0)
    with scope("q1a"):
        project_q(1, (0, 1, -1, 2, -2, 3, -3), True)
        make_q(0, 1)
    with scope("d4"):
        ring_q[1].step(4)
    with scope("q1b"):
        project_q(1, (4,))
        make_q(1, 0)

    def backward1(i, _):
        with scope("bwd"):
            backward(1, 4 + i)

        def g(t):
            def work():
                with scope("g"):
                    rs_step(0, t)

            return work

        def last():
            g(3)()
            with scope("f1"):
                ring_kv[1].step(1)

        in_order(i, i0=g(1), i1=g(2), i2=last)
        return 0

    lax.fori_loop(0, 4, backward1, 0)
    rs_step(1, 0)
    with scope("g4"):
        rs_step(0, 4)
    make_q(1, 1)
    with scope("f2"):
        ring_kv[1].step(2)
    with scope("g1"):
        rs_step(1, 1)
    with scope("f3"):
        ring_kv[1].step(3)
    with scope("g2"):
        rs_step(1, 2)
    with scope("f4"):
        ring_kv[1].step(4)
    with scope("t1"):
        transposed(1, (1,))
    with scope("g3"):
        rs_step(1, 3)

    for j in range(2):
        def forward_step(i, _):
            with scope("fwd"):
                forward(j, 4 * j + i)
            return 0

        lax.fori_loop(0, 4, forward_step, 0)

    mix_swap = to_partner(mix.at[:, theirs, :], mixed.at[pl.ds(8 * h, 8)], 9)
    mix_swap.start()

    def dn_copy(p):
        return to_partner(dnsend.at[p], dnrecv.at[p], 10 + p)

    def unrotated(x):
        return rotated(x, -1.0).astype(BF16)

    with scope("dq"):
        dq_all = [
            jnp.concatenate([unrotated(qnat[4 * j + r].astype(F32)) for r in range(4)], axis=1) for j in range(2)
        ]
    with scope("g4"):
        rs_step(1, 4)
    with scope("dkv"):
        parts = []
        for k in range(2):
            for j in range(2):
                part = dkv[j, k, at_z, :]
                for way in range(2):
                    part = part + landed[j, k, way, rs_hops[k][way] - 1].astype(F32)
                part = part.astype(BF16).astype(F32)
                part = jnp.concatenate([part, jnp.zeros((LANES - pair, HEAD_DIM), F32)], axis=0)
                parts.append(unrotated(part) if k == 0 else part.astype(BF16))
        dkv_all = jnp.concatenate(parts, axis=1)

    def dn_step(p, _):
        dnown[p] = dot_nt(dq_all[0], wqb[0, p]) + dot_nt(dq_all[1], wqb[1, p]) + dot_nt(dkv_all, wkvb[p])
        dnsend[p] = dnown[p, theirs, :].astype(BF16)
        dn_copy(p).start()
        return 0

    with scope("dn"):
        lax.fori_loop(0, planes, dn_step, 0)

    def out_copy(which, p):
        at = pl.ds(p * width, width)
        src, dst, to = ((fout, next_out, following), (gout, grad_out, preceding))[which]
        return remote(
            src.at[:, at], dst.at[:, at], out_send.at[which, p], out_recv.at[which, p], section=to
        )

    with scope("out"):
        for n in range(8):
            mixed[8 * h + n] = mix[n, mine, :]
        mix_swap.wait_recv()
        heads_all = jnp.concatenate([mixed[n] for n in range(16)], axis=1)
        for n in range(planes):
            at = pl.ds(n * width, width)
            fout[:, at] = (xf_in[:, at].astype(F32) + dot(heads_all, wo[:, at])).astype(BF16)
            out_copy(0, n).start()

    x = xs_in[...].astype(F32)
    inverse = lax.rsqrt(jnp.mean(x * x, axis=-1, keepdims=True) + norm_eps)
    along = jnp.zeros((rows, 1), F32)
    with scope("dnwait"):
        for p in range(planes):
            dn_copy(p).wait_recv()
            at = slice(p * width, (p + 1) * width)
            d = (dnown[p, mine, :] + dnrecv[p].astype(F32)).astype(BF16).astype(F32) * gain_in[:, at]
            dnown[p, mine, :] = d
            along += jnp.sum(d * x[:, at], axis=-1, keepdims=True)
    pull = along * (1.0 / x.shape[1]) * (inverse * inverse * inverse)
    with scope("grad"):
        for p in range(planes):
            at = slice(p * width, (p + 1) * width)
            grad = (dnown[p, mine, :] * inverse - x[:, at] * pull).astype(BF16)
            gout[:, at] = grad + dy_in[:, at]
            out_copy(1, p).start()

    with scope("sent"):
        for c in (*swap, mix_swap):
            c.wait_send()
        for ring in (ring_wkv, *ring_q, *ring_kv):
            ring.sent()
        for j in range(2):
            for k in range(2):
                for way in range(2):
                    for t in range(rs_hops[k][way]):
                        rs_copy(j, k, way, t).wait_send()
        for p in range(planes):
            dn_copy(p).wait_send()
    with scope("outs"):
        for which in range(2):
            for p in range(planes):
                out_copy(which, p).wait()


def shards(planes, xf, xs, dy, positions, gain, wq, wkv, wo):
    rows, features = xf.shape[1:]
    keys = 2 * planes * rows
    width = features // planes
    frequency = rope_base ** (-2.0 * jnp.arange(HEAD_DIM // 2, dtype=F32) / HEAD_DIM)
    where = positions.astype(F32)
    angles = where[:, None] * frequency[None, :]
    cos_table, sin_table = jnp.cos(angles), jnp.sin(angles)
    tables = jnp.stack(
        [
            jnp.concatenate([cos_table, cos_table], axis=1),
            jnp.concatenate([-sin_table, sin_table], axis=1),
        ]
    )
    pos_tile = jnp.broadcast_to(jnp.pad(where, (0, 128 - rows))[None, :], (8, 128))
    vmem = pl.BlockSpec(memory_space=pltpu.VMEM)
    hbm = pl.BlockSpec(memory_space=pl.ANY)
    far = planes // 2
    dma = pltpu.SemaphoreType.DMA
    out = jax.ShapeDtypeStruct((rows, features), BF16)
    produced, grads = pl.pallas_call(
        functools.partial(tick, planes, rows),
        out_shape=(out, out),
        in_specs=[vmem] * 6 + [hbm] * 3,
        out_specs=(vmem, vmem),
        scratch_shapes=[
            pltpu.VMEM((planes, width, 512), BF16),
            pltpu.VMEM((2, planes, width, 512), BF16),
            pltpu.VMEM((features, features), BF16),
            pltpu.VMEM((3, LANES, features), BF16),
            pltpu.VMEM((2, LANES, HEAD_DIM), F32),
            pltpu.VMEM((2 * planes, 8, 128), F32),
            pltpu.VMEM((planes, 2 * LANES, width), BF16),
            pltpu.VMEM((LANES, 512), F32),
            pltpu.VMEM((2, 2 * LANES, 512), F32),
            pltpu.VMEM((8, LANES, HEAD_DIM), BF16),
            pltpu.VMEM((2, 8, HEAD_DIM, LANES), BF16),
            pltpu.VMEM((2, 2, 2, keys, HEAD_DIM), BF16),
            pltpu.VMEM((2, 2, HEAD_DIM, keys), BF16),
            pltpu.VMEM((2, 2, keys, HEAD_DIM), F32),
            pltpu.VMEM((keys, LANES), F32),
            pltpu.VMEM((8, HEAD_DIM, LANES), BF16),
            pltpu.VMEM((keys, LANES), F32),
            pltpu.VMEM((keys, LANES), BF16),
            pltpu.VMEM((keys, LANES), BF16),
            pltpu.VMEM((2, 2, 2, far, 2 * rows, HEAD_DIM), BF16),
            pltpu.VMEM((2, 2, 2, far, 2 * rows, HEAD_DIM), BF16),
            pltpu.VMEM((8, LANES, HEAD_DIM), BF16),
            pltpu.VMEM((16, rows, HEAD_DIM), BF16),
            pltpu.VMEM((planes, rows, width), BF16),
            pltpu.VMEM((planes, rows, width), BF16),
            pltpu.VMEM((planes, LANES, width), F32),
            pltpu.VMEM((rows, features), BF16),
            pltpu.VMEM((rows, features), BF16),
            dma((6,)),
            dma((10 + planes,)),
            dma((10 + planes,)),
            dma((5, 3, 2, far)),
            dma((5, 3, 2, far)),
            dma((2, 2, 2, far)),
            dma((2, 2, 2, far)),
            dma((2, planes)),
            dma((2, planes)),
        ],
        compiler_params=pltpu.CompilerParams(
            collective_id=0, has_side_effects=True, vmem_limit_bytes=67_043_328
        ),
        name="tick",
    )(xs[0], xf[0], dy[0], pos_tile, tables, gain, wq[0], wkv[0], wo[0])
    return produced[None], grads[None]


def solution(mesh):
    placed = (
        P("section", "ctx", None),
        P("section", "ctx", None),
        P("section", "ctx", None),
        P("ctx"),
        P("section", None),
        P("section", "ctx", None),
        P("section", "ctx", None),
        P("section", None, None),
    )
    return jax.shard_map(
        functools.partial(shards, mesh.shape["ctx"] // 2),
        mesh=mesh,
        in_specs=placed,
        out_specs=(P("section", "ctx", None), P("section", "ctx", None)),
        check_vma=False,
    )
```

time: 209 us -> 181 us (0.87)
  starting transfers between devices: 18.4 us -> 0 us
  waiting for transfers between devices: 10.3 us -> 0 us
  local copies, waits for them, and re-layouts: 2.13 us -> 4.24 us
    ppermute x2 -> x0, starting transfers between devices: 18.4 us -> none  [from_behind(): return lax.ppermute(block, axis, route)]
    ppermute x2 -> x0, waiting for transfers between devices: 10.3 us -> none  [from_behind(): return lax.ppermute(block, axis, route)]
    unnamed x2, local copies, waits for them, and re-layouts: 1.54 us -> 3.64 us
  transfers between devices with their start and end apart: 2 -> 0, of which waited for: 1 -> 0; matrix products, arithmetic and copies ran while one was open for 0% -> 0% of each run, Pallas kernels for 0% -> 0%
where the time goes in v2:
time: 181 us; the launch traced here: 180 us
  Pallas kernels  173 us (96%)
  local copies, waits for them, and re-layouts  4.24 us (2%)
    pallas_call x1, Pallas kernels, shards(): pl.pallas_call(functools.partial(tick, planes, rows), out_shape=(out, out...  173 us
    unnamed x2, local copies, waits for them, and re-layouts  3.64 us

profile of v2, /device:TPU:1, one launch (start us, length us, event | category | flops | bytes accessed | tf_op | source)
XLA Modules:
  0.0 180.0 jit_solution(2994448243319547304)
XLA Ops:
  0.6 0.7 convert_element_type.5
  1.3 0.6 broadcast_in_dim.6.pos_in
  1.9 0.3 multiply_cosine_fusion
  2.2 0.1 maximum_bitcast_fusion
  2.3 0.7 pad_maximum_fusion.tab_in
  2.9 173.4 %tick.1 = (bf16[112,2048]{1,0:T(8,128)(2,1)}, bf16[112,2048]{1,0:T(8,128)(2,1)}) custom-call(bf16[112,2048]{1,0:T(8,128)(2,1)} %bitcast.16, bf16[112,2048]{1,0:T(8,128)(2,1)} %bitcast.17, bf16[112,2048]{1,0:T(8,128)(2,1)} %bitcast.18, f32[8,128]{1,0:T(8,128)} %broadcast_in_dim.6.pos_in, f32[2,112,128]{2,1,0:T(8,128)} %pad_maximum_fusion.tab_in, ...), custom_call_target="tpu_custom_call" | custom-call | tf_op jit(solution)/shard_map/tick/pallas_call | solution.py:627
  176.4 1.8 %copy.12 = bf16[1,112,2048]{2,1,0:T(8,128)(2,1)} copy(bf16[1,112,2048]{2,1,0:T(8,128)(2,1)} %bitcast.15) | data formatting | bytes 917504
  178.2 1.8 %copy.13 = bf16[1,112,2048]{2,1,0:T(8,128)(2,1)} copy(bf16[1,112,2048]{2,1,0:T(8,128)(2,1)} %bitcast.14) | data formatting | bytes 917504
  (2 shorter events, 0.0 us)

commit v3 on v2

--- a/solution.py
+++ b/solution.py
@@ -72,6 +72,10 @@
     dnown,
     fout,
     gout,
+    wlent,
+    last,
+    lastrecv,
+    passing,
     loc_sem,
     x_send,
     x_recv,
@@ -79,8 +83,12 @@
     ring_recv,
     rs_send,
     rs_recv,
+    mix_send,
+    mix_recv,
     out_send,
     out_recv,
+    relay_send,
+    relay_recv,
 ):
     me = lax.axis_index("ctx")
     section = lax.axis_index("section")
@@ -109,6 +117,38 @@
     for other in (following, preceding):
         pl.semaphore_signal(barrier, inc=1, device_id={"section": other}, device_id_type=MESH)
 
+    relayed = sections > 1
+    core = section % 2
+    x_hi = (section // 2) % 2
+    base = section - section % 4
+
+    def x_down(hi):
+        return h * hi + (1 - h) * (1 - hi)
+
+    def x_up(hi):
+        return (1 - h) * hi + h * (1 - hi)
+
+    relay = base + 2 * x_down(x_hi)
+    source = base + 2 * x_up(x_hi)
+    end = (source + sections - 1) % sections
+    ahead = following - following % 4 + 2 * x_down((following // 2) % 2)
+
+    def greet(to):
+        pl.semaphore_signal(
+            barrier, inc=1, device_id={"section": to, "ctx": partner}, device_id_type=MESH
+        )
+
+    if relayed:
+
+        @pl.when(core == 0)
+        def _():
+            for to in (relay, source, end):
+                greet(to)
+
+        @pl.when(core == 1)
+        def _():
+            greet(ahead)
+
     def local(src, dst, n):
         return pltpu.make_async_copy(src, dst, loc_sem.at[n])
 
@@ -141,8 +181,23 @@
     load_wo = local(wo_hbm, wo, 4)
     load_wo.start()
 
+    for n in range(3):
+        xbuf[n, pl.ds(pair, LANES - pair), :] = jnp.zeros((LANES - pair, xbuf.shape[2]), BF16)
+    for n in range(2):
+        tabs[n, pl.ds(pair, LANES - pair), :] = jnp.zeros((LANES - pair, HEAD_DIM), F32)
+    for n, src in enumerate((xs_in, xf_in, dy_in)):
+        xbuf[n, mine, :] = src[...]
+    tabs[:, mine, :] = tab_in[...]
+    for n in range(2):
+        for k in range(2):
+            dkv[n, k] = jnp.zeros((keys, HEAD_DIM), F32)
+
     with scope("barrier"):
-        pl.semaphore_wait(barrier, 5)
+        if relayed:
+            pl.when(core == 0)(lambda: pl.semaphore_wait(barrier, 8))
+            pl.when(core == 1)(lambda: pl.semaphore_wait(barrier, 6))
+        else:
+            pl.semaphore_wait(barrier, 5)
 
     given = pieces(1 - h)
     tokens = [(src, xbuf.at[n, mine, :]) for n, src in enumerate((xs_in, xf_in, dy_in))]
@@ -167,8 +222,10 @@
             sems = (self.number, n, way, t)
             return remote(block, block, ring_send.at[sems], ring_recv.at[sems], ctx=to_z[way])
 
-        def step(self, t, ready=None):
+        def step(self, t, ready=None, only=None):
             for n, (_, *hops) in enumerate(self.parts):
+                if only is not None and n != only:
+                    continue
                 if t == 0 and ready is not None:
                     ready(n)
                 for way in range(2):
@@ -367,19 +424,15 @@
         for name, work in steps.items():
             pl.when(i == int(name[1:]))(work)
 
-    for n in range(3):
-        xbuf[n, pl.ds(pair, LANES - pair), :] = jnp.zeros((LANES - pair, xbuf.shape[2]), BF16)
-    for n in range(2):
-        tabs[n, pl.ds(pair, LANES - pair), :] = jnp.zeros((LANES - pair, HEAD_DIM), F32)
-    for n, src in enumerate((xs_in, xf_in, dy_in)):
-        xbuf[n, mine, :] = src[...]
-    tabs[:, mine, :] = tab_in[...]
-    for n in range(2):
-        for k in range(2):
-            dkv[n, k] = jnp.zeros((keys, HEAD_DIM), F32)
+    def lend(k):
+        at = pl.ds(256 * k + 128, 128)
+        return to_partner(wkvb.at[:, :, at], wlent.at[:, :, pl.ds(128 * k, 128)], 10 + k)
 
     with scope("a0"):
-        ring_wkv.step(0, ready_wkv)
+        ring_wkv.step(0, ready_wkv, 0)
+        ring_q[0].step(0, ready_q(0), 0)
+        ring_wkv.step(0, ready_wkv, 1)
+        ring_wkv.step(0, ready_wkv, 2)
     with scope("a1"):
         ring_wkv.step(1)
     with scope("a2"):
@@ -387,41 +440,39 @@
     with scope("a3"):
         ring_wkv.step(3)
     with scope("c0"):
-        ring_q[0].step(0, ready_q(0))
+        ring_q[0].step(0, ready_q(0), 1)
     with scope("norms0"):
         swap[3].wait_recv()
         swap[4].wait_recv()
         norms(0)
     with scope("a4"):
         ring_wkv.step(4)
+    for k in range(2):
+        lend(k).start()
     with scope("kv0"):
         project_kv(0)
         make_kv(0)
     ring_kv[0].step(0)
-    with scope("norms1"):
-        swap[7].wait_recv()
-        norms(1)
     with scope("c1"):
         ring_q[0].step(1)
-    with scope("q0a"):
-        project_q(0, (0, 1, -1), True)
     with scope("b1"):
         ring_kv[0].step(1)
     with scope("bias"):
         make_bias()
     with scope("c2"):
         ring_q[0].step(2)
-    with scope("q0b"):
-        project_q(0, (2, -2))
     with scope("b2"):
         ring_kv[0].step(2)
+    with scope("norms1"):
+        swap[7].wait_recv()
+        norms(1)
     with scope("kv1"):
         project_kv(1)
         make_kv(1)
     with scope("c3"):
         ring_q[0].step(3)
     with scope("q0c"):
-        project_q(0, (3, -3))
+        project_q(0, (0, 1, -1, 2, -2, 3, -3), True)
     with scope("b3"):
         ring_kv[0].step(3)
     ring_q[1].step(0, ready_q(1))
@@ -438,23 +489,21 @@
         ring_kv[0].step(4)
     with scope("t0"):
         transposed(0, (0, 1))
-    with scope("d1"):
-        ring_q[1].step(1)
 
     def backward0(i, _):
         with scope("bwd"):
             backward(0, i)
 
-        def first():
-            with scope("d2"):
-                ring_q[1].step(2)
-
-        def second():
-            with scope("d3"):
-                ring_q[1].step(3)
-            ring_kv[1].step(0)
-
-        in_order(i, i1=first, i3=second)
+        def d(t):
+            def work():
+                with scope("d"):
+                    ring_q[1].step(t)
+                    if t == 3:
+                        ring_kv[1].step(0)
+
+            return work
+
+        in_order(i, i0=d(1), i2=d(2), i3=d(3))
         return 0
 
     lax.fori_loop(0, 4, backward0, 0)
@@ -476,80 +525,90 @@
             def work():
                 with scope("g"):
                     rs_step(0, t)
+                with scope("f"):
+                    ring_kv[1].step(t)
 
             return work
 
-        def last():
-            g(3)()
-            with scope("f1"):
-                ring_kv[1].step(1)
-
-        in_order(i, i0=g(1), i1=g(2), i2=last)
+        in_order(i, i0=g(1), i1=g(2), i2=g(3))
         return 0
 
     lax.fori_loop(0, 4, backward1, 0)
     rs_step(1, 0)
     with scope("g4"):
         rs_step(0, 4)
-    make_q(1, 1)
-    with scope("f2"):
-        ring_kv[1].step(2)
-    with scope("g1"):
-        rs_step(1, 1)
-    with scope("f3"):
-        ring_kv[1].step(3)
-    with scope("g2"):
-        rs_step(1, 2)
+
+    def unrotated(x):
+        return rotated(x, -1.0).astype(BF16)
+
+    def owned(j):
+        parts = []
+        for k in range(2):
+            part = dkv[j, k, at_z, :]
+            for way in range(2):
+                part = part + landed[j, k, way, rs_hops[k][way] - 1].astype(F32)
+            part = part.astype(BF16).astype(F32)
+            part = jnp.concatenate([part, jnp.zeros((LANES - pair, HEAD_DIM), F32)], axis=0)
+            parts.append(unrotated(part) if k == 0 else part.astype(BF16))
+        return jnp.concatenate(parts, axis=1)
+
+    def dn_copy(p):
+        return to_partner(dnsend.at[p], dnrecv.at[p], 14 + p)
+
+    with scope("dq"):
+        dq_all = [
+            jnp.concatenate([unrotated(qnat[4 * j + r].astype(F32)) for r in range(4)], axis=1) for j in range(2)
+        ]
+        dkv0 = owned(0)
+
+    def first_w(p):
+        return jnp.concatenate([wkvb[p, :, 0:128], wkvb[p, :, 256:384]], axis=1)
+
+    def second_w(p):
+        return jnp.concatenate([wkvb[p, :, 128:256], wkvb[p, :, 384:512]], axis=1)
+
+    def dn_step(p, _):
+        dnown[p] = dot_nt(dq_all[0], wqb[0, p]) + dot_nt(dq_all[1], wqb[1, p]) + dot_nt(dkv0, first_w(p))
+        dnsend[p] = dnown[p, theirs, :].astype(BF16)
+        dn_copy(p).start()
+        return 0
+
+    with scope("dn"):
+        lax.fori_loop(0, planes, dn_step, 0)
     with scope("f4"):
         ring_kv[1].step(4)
     with scope("t1"):
         transposed(1, (1,))
-    with scope("g3"):
-        rs_step(1, 3)
-
-    for j in range(2):
-        def forward_step(i, _):
-            with scope("fwd"):
-                forward(j, 4 * j + i)
-            return 0
-
-        lax.fori_loop(0, 4, forward_step, 0)
-
-    mix_swap = to_partner(mix.at[:, theirs, :], mixed.at[pl.ds(8 * h, 8)], 9)
-    mix_swap.start()
-
-    def dn_copy(p):
-        return to_partner(dnsend.at[p], dnrecv.at[p], 10 + p)
-
-    def unrotated(x):
-        return rotated(x, -1.0).astype(BF16)
-
-    with scope("dq"):
-        dq_all = [
-            jnp.concatenate([unrotated(qnat[4 * j + r].astype(F32)) for r in range(4)], axis=1) for j in range(2)
-        ]
+        make_q(1, 1)
+
+    def mix_copy(i):
+        return remote(
+            mix.at[i, theirs, :], mixed.at[8 * h + i], mix_send.at[i], mix_recv.at[i], ctx=partner
+        )
+
+    def forward_step(i, _):
+        with scope("fwd"):
+            forward(i // 4, i)
+        mix_copy(i).start()
+
+        def g(t):
+            def work():
+                with scope("g"):
+                    rs_step(1, t)
+
+            return work
+
+        in_order(i, i1=g(1), i4=g(2), i6=g(3))
+        return 0
+
+    lax.fori_loop(0, 8, forward_step, 0)
+
     with scope("g4"):
         rs_step(1, 4)
     with scope("dkv"):
-        parts = []
-        for k in range(2):
-            for j in range(2):
-                part = dkv[j, k, at_z, :]
-                for way in range(2):
-                    part = part + landed[j, k, way, rs_hops[k][way] - 1].astype(F32)
-                part = part.astype(BF16).astype(F32)
-                part = jnp.concatenate([part, jnp.zeros((LANES - pair, HEAD_DIM), F32)], axis=0)
-                parts.append(unrotated(part) if k == 0 else part.astype(BF16))
-        dkv_all = jnp.concatenate(parts, axis=1)
-
-    def dn_step(p, _):
-        dnown[p] = dot_nt(dq_all[0], wqb[0, p]) + dot_nt(dq_all[1], wqb[1, p]) + dot_nt(dkv_all, wkvb[p])
-        dnsend[p] = dnown[p, theirs, :].astype(BF16)
-        dn_copy(p).start()
-        return 0
-
-    with scope("dn"):
-        lax.fori_loop(0, planes, dn_step, 0)
+        last[...] = owned(1)
+    last_swap = to_partner(last.at[theirs, :], lastrecv, 12)
+    last_swap.start()
 
     def out_copy(which, p):
         at = pl.ds(p * width, width)
@@ -558,10 +617,32 @@
             src.at[:, at], dst.at[:, at], out_send.at[which, p], out_recv.at[which, p], section=to
         )
 
+    by_relay = (0, 2, 4, 6)
+
+    def relay_in(p):
+        at = pl.ds(p * width, width)
+        return remote(
+            gout.at[:, at], passing.at[p], out_send.at[1, p], relay_recv.at[p], section=relay, ctx=partner
+        )
+
+    def relay_out(p):
+        at = pl.ds(p * width, width)
+        return remote(
+            passing.at[p], grad_out.at[:, at], relay_send.at[p], out_recv.at[1, p], section=end, ctx=partner
+        )
+
+    def send_grad(p):
+        if relayed and p in by_relay:
+            pl.when(core == 0)(lambda: relay_in(p).start())
+            pl.when(core == 1)(lambda: out_copy(1, p).start())
+        else:
+            out_copy(1, p).start()
+
     with scope("out"):
         for n in range(8):
             mixed[8 * h + n] = mix[n, mine, :]
-        mix_swap.wait_recv()
+        for n in range(8):
+            mix_copy(n).wait_recv()
         heads_all = jnp.concatenate([mixed[n] for n in range(16)], axis=1)
         for n in range(planes):
             at = pl.ds(n * width, width)
@@ -574,8 +655,16 @@
     with scope("dnwait"):
         for p in range(planes):
             dn_copy(p).wait_recv()
+        for k in range(2):
+            lend(k).wait_recv()
+        last_swap.wait_recv()
+    with scope("last"):
+        own_last = last[mine, :]
+        for p in range(planes):
             at = slice(p * width, (p + 1) * width)
-            d = (dnown[p, mine, :] + dnrecv[p].astype(F32)).astype(BF16).astype(F32) * gain_in[:, at]
+            total = dnown[p, mine, :] + dnrecv[p].astype(F32)
+            total += dot_nt(own_last, second_w(p)) + dot_nt(lastrecv[...], wlent[p])
+            d = total.astype(BF16).astype(F32) * gain_in[:, at]
             dnown[p, mine, :] = d
             along += jnp.sum(d * x[:, at], axis=-1, keepdims=True)
     pull = along * (1.0 / x.shape[1]) * (inverse * inverse * inverse)
@@ -584,10 +673,19 @@
             at = slice(p * width, (p + 1) * width)
             grad = (dnown[p, mine, :] * inverse - x[:, at] * pull).astype(BF16)
             gout[:, at] = grad + dy_in[:, at]
-            out_copy(1, p).start()
+            send_grad(p)
+
+    if relayed:
+
+        @pl.when(core == 0)
+        def _():
+            with scope("relay"):
+                for p in by_relay:
+                    relay_in(p).wait_recv()
+                    relay_out(p).start()
 
     with scope("sent"):
-        for c in (*swap, mix_swap):
+        for c in (*swap, last_swap, lend(0), lend(1), *(mix_copy(n) for n in range(8))):
             c.wait_send()
         for ring in (ring_wkv, *ring_q, *ring_kv):
             ring.sent()
@@ -602,6 +700,12 @@
         for which in range(2):
             for p in range(planes):
                 out_copy(which, p).wait()
+        if relayed:
+
+            @pl.when(core == 0)
+            def _():
+                for p in by_relay:
+                    relay_out(p).wait_send()
 
 
 def shards(planes, xf, xs, dy, positions, gain, wq, wkv, wo):
@@ -658,15 +762,23 @@
             pltpu.VMEM((planes, LANES, width), F32),
             pltpu.VMEM((rows, features), BF16),
             pltpu.VMEM((rows, features), BF16),
+            pltpu.VMEM((planes, width, 256), BF16),
+            pltpu.VMEM((LANES, 256), BF16),
+            pltpu.VMEM((rows, 256), BF16),
+            pltpu.VMEM((planes, rows, width), BF16),
             dma((6,)),
-            dma((10 + planes,)),
-            dma((10 + planes,)),
+            dma((14 + planes,)),
+            dma((14 + planes,)),
             dma((5, 3, 2, far)),
             dma((5, 3, 2, far)),
             dma((2, 2, 2, far)),
             dma((2, 2, 2, far)),
+            dma((8,)),
+            dma((8,)),
             dma((2, planes)),
             dma((2, planes)),
+            dma((planes,)),
+            dma((planes,)),
         ],
         compiler_params=pltpu.CompilerParams(
             collective_id=0, has_side_effects=True, vmem_limit_bytes=67_043_328

time: 181 us -> 167 us (0.923)
  Pallas kernels: 173 us -> 161 us
    pallas_call x1, Pallas kernels: 173 us -> 161 us  [shards(): pl.pallas_call(functools.partial(tick, planes, rows), out_shape=(out, out...]
where the time goes in v3:
time: 167 us
  Pallas kernels  161 us (96%)
  local copies, waits for them, and re-layouts  4.24 us (3%)
  other arithmetic  1.7 us (1%)
    pallas_call x1, Pallas kernels, shards(): pl.pallas_call(functools.partial(tick, planes, rows), out_shape=(out, out...  161 us
    unnamed x2, local copies, waits for them, and re-layouts  3.64 us

profile of v3, /device:TPU:1, one launch (start us, length us, event | category | flops | bytes accessed | tf_op | source)
XLA Modules:
  0.0 167.1 jit_solution(14512909290431530357)
XLA Ops:
  0.6 0.7 convert_element_type.5
  1.3 0.6 broadcast_in_dim.6.pos_in
  1.9 0.3 multiply_cosine_fusion
  2.2 0.1 maximum_bitcast_fusion
  2.3 0.7 pad_maximum_fusion.tab_in
  2.9 160.5 %tick.1 = (bf16[112,2048]{1,0:T(8,128)(2,1)}, bf16[112,2048]{1,0:T(8,128)(2,1)}) custom-call(bf16[112,2048]{1,0:T(8,128)(2,1)} %bitcast.16, bf16[112,2048]{1,0:T(8,128)(2,1)} %bitcast.17, bf16[112,2048]{1,0:T(8,128)(2,1)} %bitcast.18, f32[8,128]{1,0:T(8,128)} %broadcast_in_dim.6.pos_in, f32[2,112,128]{2,1,0:T(8,128)} %pad_maximum_fusion.tab_in, ...), custom_call_target="tpu_custom_call" | custom-call | tf_op jit(solution)/shard_map/tick/pallas_call | solution.py:731
  163.5 1.8 %copy.12 = bf16[1,112,2048]{2,1,0:T(8,128)(2,1)} copy(bf16[1,112,2048]{2,1,0:T(8,128)(2,1)} %bitcast.15) | data formatting | bytes 917504
  165.3 1.8 %copy.13 = bf16[1,112,2048]{2,1,0:T(8,128)(2,1)} copy(bf16[1,112,2048]{2,1,0:T(8,128)(2,1)} %bitcast.14) | data formatting | bytes 917504
  (2 shorter events, 0.0 us)

commit v4 on v3

--- a/solution.py
+++ b/solution.py
@@ -2,6 +2,7 @@
 
 import jax
 import jax.numpy as jnp
+import numpy as np
 from jax import lax
 from jax.experimental import pallas as pl
 from jax.experimental.pallas import tpu as pltpu
@@ -37,7 +38,7 @@
     xf_in,
     dy_in,
     pos_in,
-    tab_in,
+    freq_in,
     gain_in,
     wq_hbm,
     wkv_hbm,
@@ -50,6 +51,7 @@
     xbuf,
     tabs,
     posb,
+    posown,
     normed,
     acc_kv,
     acc_q,
@@ -75,7 +77,6 @@
     wlent,
     last,
     lastrecv,
-    passing,
     loc_sem,
     x_send,
     x_recv,
@@ -87,8 +88,6 @@
     mix_recv,
     out_send,
     out_recv,
-    relay_send,
-    relay_recv,
 ):
     me = lax.axis_index("ctx")
     section = lax.axis_index("section")
@@ -107,47 +106,21 @@
     chunks = keys // chunk
     far = planes // 2
     mine = pl.ds(pl.multiple_of(h * rows, 16), rows)
-    theirs = pl.ds(pl.multiple_of((1 - h) * rows, 16), rows)
     scale = HEAD_DIM ** (-0.5)
     scope = jax.named_scope
 
     barrier = pltpu.get_barrier_semaphore()
     for other in (partner, *to_z):
         pl.semaphore_signal(barrier, inc=1, device_id={"ctx": other}, device_id_type=MESH)
-    for other in (following, preceding):
-        pl.semaphore_signal(barrier, inc=1, device_id={"section": other}, device_id_type=MESH)
-
-    relayed = sections > 1
     core = section % 2
-    x_hi = (section // 2) % 2
-    base = section - section % 4
-
-    def x_down(hi):
-        return h * hi + (1 - h) * (1 - hi)
-
-    def x_up(hi):
-        return (1 - h) * hi + h * (1 - hi)
-
-    relay = base + 2 * x_down(x_hi)
-    source = base + 2 * x_up(x_hi)
-    end = (source + sections - 1) % sections
-    ahead = following - following % 4 + 2 * x_down((following // 2) % 2)
-
-    def greet(to):
-        pl.semaphore_signal(
-            barrier, inc=1, device_id={"section": to, "ctx": partner}, device_id_type=MESH
-        )
-
-    if relayed:
-
-        @pl.when(core == 0)
-        def _():
-            for to in (relay, source, end):
-                greet(to)
-
-        @pl.when(core == 1)
-        def _():
-            greet(ahead)
+    f_side = core * (1 - h) + (1 - core) * h
+    g_side = core * h + (1 - core) * (1 - h)
+    f_rows, f_other = (pl.ds(pl.multiple_of(n * rows, 16), rows) for n in (f_side, 1 - f_side))
+    g_rows, g_other = (pl.ds(pl.multiple_of(n * rows, 16), rows) for n in (g_side, 1 - g_side))
+    f_to = {"section": following, "ctx": z * 2 + f_side}
+    g_to = {"section": preceding, "ctx": z * 2 + g_side}
+    for other in (f_to, g_to):
+        pl.semaphore_signal(barrier, inc=1, device_id=other, device_id_type=MESH)
 
     def local(src, dst, n):
         return pltpu.make_async_copy(src, dst, loc_sem.at[n])
@@ -175,36 +148,32 @@
 
     my_rows = pl.ds(pl.multiple_of(h * half, 128), half)
     own = [local(src, dst, n) for n, (src, dst) in enumerate(pieces(h))]
-    keep_pos = local(pos_in, posb.at[me], 5)
-    for c in (*own, keep_pos):
+    for c in own:
         c.start()
     load_wo = local(wo_hbm, wo, 4)
     load_wo.start()
 
     for n in range(3):
         xbuf[n, pl.ds(pair, LANES - pair), :] = jnp.zeros((LANES - pair, xbuf.shape[2]), BF16)
-    for n in range(2):
-        tabs[n, pl.ds(pair, LANES - pair), :] = jnp.zeros((LANES - pair, HEAD_DIM), F32)
+    tabs[:, pl.ds(pair, LANES - pair), :] = jnp.zeros((2, LANES - pair, HEAD_DIM), F32)
+    where = jnp.concatenate([pos_in[...].astype(F32), jnp.zeros((1, 128 - rows), F32)], axis=1)
+    posown[...] = jnp.broadcast_to(where, (8, 128))
     for n, src in enumerate((xs_in, xf_in, dy_in)):
         xbuf[n, mine, :] = src[...]
-    tabs[:, mine, :] = tab_in[...]
     for n in range(2):
         for k in range(2):
             dkv[n, k] = jnp.zeros((keys, HEAD_DIM), F32)
 
+    posb[me] = posown[...]
+
     with scope("barrier"):
-        if relayed:
-            pl.when(core == 0)(lambda: pl.semaphore_wait(barrier, 8))
-            pl.when(core == 1)(lambda: pl.semaphore_wait(barrier, 6))
-        else:
-            pl.semaphore_wait(barrier, 5)
+        pl.semaphore_wait(barrier, 5)
 
     given = pieces(1 - h)
     tokens = [(src, xbuf.at[n, mine, :]) for n, src in enumerate((xs_in, xf_in, dy_in))]
     swaps = [
         *given[:2],
-        (pos_in, posb.at[me]),
-        (tab_in, tabs.at[:, mine, :]),
+        (posown, posb.at[me]),
         tokens[0],
         *given[2:],
         *tokens[1:],
@@ -267,7 +236,6 @@
             swap[0].wait_recv()
             swap[1].wait_recv()
         else:
-            keep_pos.wait()
             swap[2].wait_recv()
 
     def ready_q(j):
@@ -275,7 +243,7 @@
             if n == 0:
                 own[2 + j].wait()
             else:
-                swap[5 + j].wait_recv()
+                swap[4 + j].wait_recv()
 
         return ready
 
@@ -316,6 +284,16 @@
 
         lax.fori_loop(0, 8, body, 0)
 
+    def make_tables():
+        lane = lax.broadcasted_iota(jnp.int32, (rows, HEAD_DIM), 1)
+        for n in range(2):
+            column = jnp.broadcast_to(posb[2 * z + n][0:1, :], (128, 128)).T[:rows]
+            angles = column * freq_in[...]
+            at = pl.ds(n * rows, rows)
+            sine = jnp.sin(angles)
+            tabs[0, at, :] = jnp.cos(angles)
+            tabs[1, at, :] = jnp.where(lane < HEAD_DIM // 2, -sine, sine)
+
     def rotated(x, sign):
         return x * tabs[0] + sign * (pltpu.roll(x, HEAD_DIM // 2, 1) * tabs[1])
 
@@ -352,8 +330,8 @@
 
         lax.fori_loop(0, 2 * planes, body, 0)
 
-    def transposed(m, ks):
-        for j in range(2):
+    def transposed(m, ks, js=(0, 1)):
+        for j in js:
             for k in ks:
                 for i in range(keys // 128):
                     at = pl.ds(i * 128, 128)
@@ -425,8 +403,8 @@
             pl.when(i == int(name[1:]))(work)
 
     def lend(k):
-        at = pl.ds(256 * k + 128, 128)
-        return to_partner(wkvb.at[:, :, at], wlent.at[:, :, pl.ds(128 * k, 128)], 10 + k)
+        at = pl.ds(k * (planes // 2), planes // 2)
+        return to_partner(wkvb.at[at], wlent.at[at], 10 + k)
 
     with scope("a0"):
         ring_wkv.step(0, ready_wkv, 0)
@@ -440,11 +418,12 @@
     with scope("a3"):
         ring_wkv.step(3)
     with scope("c0"):
+        ring_q[0].step(1, None, 0)
         ring_q[0].step(0, ready_q(0), 1)
     with scope("norms0"):
         swap[3].wait_recv()
-        swap[4].wait_recv()
         norms(0)
+        make_tables()
     with scope("a4"):
         ring_wkv.step(4)
     for k in range(2):
@@ -454,7 +433,7 @@
         make_kv(0)
     ring_kv[0].step(0)
     with scope("c1"):
-        ring_q[0].step(1)
+        ring_q[0].step(1, None, 1)
     with scope("b1"):
         ring_kv[0].step(1)
     with scope("bias"):
@@ -464,7 +443,7 @@
     with scope("b2"):
         ring_kv[0].step(2)
     with scope("norms1"):
-        swap[7].wait_recv()
+        swap[6].wait_recv()
         norms(1)
     with scope("kv1"):
         project_kv(1)
@@ -478,7 +457,7 @@
     ring_q[1].step(0, ready_q(1))
     with scope("dm"):
         load_wo.wait()
-        swap[8].wait_recv()
+        swap[7].wait_recv()
         grads_in()
     with scope("c4"):
         ring_q[0].step(4)
@@ -490,23 +469,25 @@
     with scope("t0"):
         transposed(0, (0, 1))
 
+    def d_step(t, n):
+        with scope(f"d{t}{n}"):
+            ring_q[1].step(t, None, n)
+
+    d_step(1, 0)
+
     def backward0(i, _):
         with scope("bwd"):
             backward(0, i)
 
-        def d(t):
-            def work():
-                with scope("d"):
-                    ring_q[1].step(t)
-                    if t == 3:
-                        ring_kv[1].step(0)
-
-            return work
-
-        in_order(i, i0=d(1), i2=d(2), i3=d(3))
+        def third():
+            d_step(2, 1)
+            d_step(3, 0)
+
+        in_order(i, i0=lambda: d_step(1, 1), i1=lambda: d_step(2, 0), i2=third, i3=lambda: d_step(3, 1))
         return 0
 
     lax.fori_loop(0, 4, backward0, 0)
+    ring_kv[1].step(0)
     rs_step(0, 0)
     with scope("q1a"):
         project_q(1, (0, 1, -1, 2, -2, 3, -3), True)
@@ -517,26 +498,29 @@
         project_q(1, (4,))
         make_q(1, 0)
 
+    def f_step(t, j):
+        with scope(f"f{t}{j}"):
+            ring_kv[1].step(t, None, j)
+
+    def g_step(j, t):
+        with scope(f"g{j}{t}"):
+            rs_step(j, t)
+
     def backward1(i, _):
         with scope("bwd"):
             backward(1, 4 + i)
 
-        def g(t):
-            def work():
-                with scope("g"):
-                    rs_step(0, t)
-                with scope("f"):
-                    ring_kv[1].step(t)
-
-            return work
-
-        in_order(i, i0=g(1), i1=g(2), i2=g(3))
+        in_order(
+            i,
+            i0=lambda: f_step(1, 0),
+            i1=lambda: f_step(1, 1),
+            i2=lambda: g_step(0, 1),
+            i3=lambda: f_step(2, 0),
+        )
         return 0
 
     lax.fori_loop(0, 4, backward1, 0)
     rs_step(1, 0)
-    with scope("g4"):
-        rs_step(0, 4)
 
     def unrotated(x):
         return rotated(x, -1.0).astype(BF16)
@@ -559,133 +543,128 @@
         dq_all = [
             jnp.concatenate([unrotated(qnat[4 * j + r].astype(F32)) for r in range(4)], axis=1) for j in range(2)
         ]
-        dkv0 = owned(0)
-
-    def first_w(p):
-        return jnp.concatenate([wkvb[p, :, 0:128], wkvb[p, :, 256:384]], axis=1)
-
-    def second_w(p):
-        return jnp.concatenate([wkvb[p, :, 128:256], wkvb[p, :, 384:512]], axis=1)
+    f_step(2, 1)
+
+    def columns(ref, p, j):
+        return jnp.concatenate(
+            [ref[p, :, 128 * j : 128 * j + 128], ref[p, :, 256 + 128 * j : 384 + 128 * j]], axis=1
+        )
 
     def dn_step(p, _):
-        dnown[p] = dot_nt(dq_all[0], wqb[0, p]) + dot_nt(dq_all[1], wqb[1, p]) + dot_nt(dkv0, first_w(p))
-        dnsend[p] = dnown[p, theirs, :].astype(BF16)
+        dnown[p] = dot_nt(dq_all[0], wqb[0, p]) + dot_nt(dq_all[1], wqb[1, p])
+        dnsend[p] = dnown[p, g_other, :].astype(BF16)
         dn_copy(p).start()
         return 0
 
+    def own_swap(j):
+        return to_partner(last.at[j, g_other, :], lastrecv.at[j], 12 + j)
+
+    def own_grads(j):
+        with scope("dkv"):
+            last[j] = owned(j)
+        own_swap(j).start()
+
+    def add_own(j):
+        own_swap(j).wait_recv()
+        own = last[j, g_rows, :]
+        for p in range(planes):
+            dnown[p, g_rows, :] += dot_nt(own, columns(wkvb, p, j)) + dot_nt(lastrecv[j], columns(wlent, p, j))
+
     with scope("dn"):
         lax.fori_loop(0, planes, dn_step, 0)
-    with scope("f4"):
-        ring_kv[1].step(4)
+    g_step(0, 2)
+    f_step(3, 0)
+    g_step(1, 1)
+    f_step(3, 1)
+    f_step(4, 0)
     with scope("t1"):
-        transposed(1, (1,))
+        transposed(1, (1,), (0,))
         make_q(1, 1)
 
     def mix_copy(i):
         return remote(
-            mix.at[i, theirs, :], mixed.at[8 * h + i], mix_send.at[i], mix_recv.at[i], ctx=partner
+            mix.at[i, f_other, :], mixed.at[8 * h + i], mix_send.at[i], mix_recv.at[i], ctx=partner
         )
 
     def forward_step(i, _):
+        def group1():
+            f_step(4, 1)
+            with scope("t1"):
+                transposed(1, (1,), (1,))
+
+        in_order(i, i4=group1)
         with scope("fwd"):
             forward(i // 4, i)
         mix_copy(i).start()
 
-        def g(t):
-            def work():
-                with scope("g"):
-                    rs_step(1, t)
-
-            return work
-
-        in_order(i, i1=g(1), i4=g(2), i6=g(3))
+        def fourth():
+            g_step(0, 4)
+            own_grads(0)
+
+        def sixth():
+            with scope("add0"):
+                for k in range(2):
+                    lend(k).wait_recv()
+                add_own(0)
+
+        in_order(
+            i,
+            i1=lambda: g_step(0, 3),
+            i2=lambda: g_step(1, 2),
+            i4=fourth,
+            i5=lambda: g_step(1, 3),
+            i6=sixth,
+        )
         return 0
 
     lax.fori_loop(0, 8, forward_step, 0)
 
     with scope("g4"):
         rs_step(1, 4)
-    with scope("dkv"):
-        last[...] = owned(1)
-    last_swap = to_partner(last.at[theirs, :], lastrecv, 12)
-    last_swap.start()
+    own_grads(1)
 
     def out_copy(which, p):
         at = pl.ds(p * width, width)
-        src, dst, to = ((fout, next_out, following), (gout, grad_out, preceding))[which]
-        return remote(
-            src.at[:, at], dst.at[:, at], out_send.at[which, p], out_recv.at[which, p], section=to
-        )
-
-    by_relay = (0, 2, 4, 6)
-
-    def relay_in(p):
-        at = pl.ds(p * width, width)
-        return remote(
-            gout.at[:, at], passing.at[p], out_send.at[1, p], relay_recv.at[p], section=relay, ctx=partner
-        )
-
-    def relay_out(p):
-        at = pl.ds(p * width, width)
-        return remote(
-            passing.at[p], grad_out.at[:, at], relay_send.at[p], out_recv.at[1, p], section=end, ctx=partner
-        )
-
-    def send_grad(p):
-        if relayed and p in by_relay:
-            pl.when(core == 0)(lambda: relay_in(p).start())
-            pl.when(core == 1)(lambda: out_copy(1, p).start())
-        else:
-            out_copy(1, p).start()
+        src, dst, to = ((fout, next_out, f_to), (gout, grad_out, g_to))[which]
+        return remote(src.at[:, at], dst.at[:, at], out_send.at[which, p], out_recv.at[which, p], **to)
 
     with scope("out"):
         for n in range(8):
-            mixed[8 * h + n] = mix[n, mine, :]
+            mixed[8 * h + n] = mix[n, f_rows, :]
         for n in range(8):
             mix_copy(n).wait_recv()
         heads_all = jnp.concatenate([mixed[n] for n in range(16)], axis=1)
         for n in range(planes):
             at = pl.ds(n * width, width)
-            fout[:, at] = (xf_in[:, at].astype(F32) + dot(heads_all, wo[:, at])).astype(BF16)
+            fout[:, at] = (xbuf[1, f_rows, at].astype(F32) + dot(heads_all, wo[:, at])).astype(BF16)
             out_copy(0, n).start()
 
-    x = xs_in[...].astype(F32)
+    x = xbuf[0, g_rows, :].astype(F32)
     inverse = lax.rsqrt(jnp.mean(x * x, axis=-1, keepdims=True) + norm_eps)
     along = jnp.zeros((rows, 1), F32)
     with scope("dnwait"):
         for p in range(planes):
             dn_copy(p).wait_recv()
-        for k in range(2):
-            lend(k).wait_recv()
-        last_swap.wait_recv()
+        own_swap(1).wait_recv()
     with scope("last"):
-        own_last = last[mine, :]
+        own_last = last[1, g_rows, :]
         for p in range(planes):
             at = slice(p * width, (p + 1) * width)
-            total = dnown[p, mine, :] + dnrecv[p].astype(F32)
-            total += dot_nt(own_last, second_w(p)) + dot_nt(lastrecv[...], wlent[p])
+            total = dnown[p, g_rows, :] + dnrecv[p].astype(F32)
+            total += dot_nt(own_last, columns(wkvb, p, 1)) + dot_nt(lastrecv[1], columns(wlent, p, 1))
             d = total.astype(BF16).astype(F32) * gain_in[:, at]
-            dnown[p, mine, :] = d
+            dnown[p, g_rows, :] = d
             along += jnp.sum(d * x[:, at], axis=-1, keepdims=True)
     pull = along * (1.0 / x.shape[1]) * (inverse * inverse * inverse)
     with scope("grad"):
         for p in range(planes):
             at = slice(p * width, (p + 1) * width)
-            grad = (dnown[p, mine, :] * inverse - x[:, at] * pull).astype(BF16)
-            gout[:, at] = grad + dy_in[:, at]
-            send_grad(p)
-
-    if relayed:
-
-        @pl.when(core == 0)
-        def _():
-            with scope("relay"):
-                for p in by_relay:
-                    relay_in(p).wait_recv()
-                    relay_out(p).start()
+            grad = (dnown[p, g_rows, :] * inverse - x[:, at] * pull).astype(BF16)
+            gout[:, at] = grad + xbuf[2, g_rows, at]
+            out_copy(1, p).start()
 
     with scope("sent"):
-        for c in (*swap, last_swap, lend(0), lend(1), *(mix_copy(n) for n in range(8))):
+        for c in (*swap, own_swap(0), own_swap(1), lend(0), lend(1), *(mix_copy(n) for n in range(8))):
             c.wait_send()
         for ring in (ring_wkv, *ring_q, *ring_kv):
             ring.sent()
@@ -700,29 +679,14 @@
         for which in range(2):
             for p in range(planes):
                 out_copy(which, p).wait()
-        if relayed:
-
-            @pl.when(core == 0)
-            def _():
-                for p in by_relay:
-                    relay_out(p).wait_send()
 
 
 def shards(planes, xf, xs, dy, positions, gain, wq, wkv, wo):
     rows, features = xf.shape[1:]
     keys = 2 * planes * rows
     width = features // planes
-    frequency = rope_base ** (-2.0 * jnp.arange(HEAD_DIM // 2, dtype=F32) / HEAD_DIM)
-    where = positions.astype(F32)
-    angles = where[:, None] * frequency[None, :]
-    cos_table, sin_table = jnp.cos(angles), jnp.sin(angles)
-    tables = jnp.stack(
-        [
-            jnp.concatenate([cos_table, cos_table], axis=1),
-            jnp.concatenate([-sin_table, sin_table], axis=1),
-        ]
-    )
-    pos_tile = jnp.broadcast_to(jnp.pad(where, (0, 128 - rows))[None, :], (8, 128))
+    frequency = rope_base ** (-2.0 * np.arange(HEAD_DIM // 2) / HEAD_DIM)
+    frequency = jnp.asarray(np.tile(frequency, 2)[None, :], F32)
     vmem = pl.BlockSpec(memory_space=pltpu.VMEM)
     hbm = pl.BlockSpec(memory_space=pl.ANY)
     far = planes // 2
@@ -732,7 +696,7 @@
         functools.partial(tick, planes, rows),
         out_shape=(out, out),
         in_specs=[vmem] * 6 + [hbm] * 3,
-        out_specs=(vmem, vmem),
+        out_specs=(hbm, hbm),
         scratch_shapes=[
             pltpu.VMEM((planes, width, 512), BF16),
             pltpu.VMEM((2, planes, width, 512), BF16),
@@ -740,6 +704,7 @@
             pltpu.VMEM((3, LANES, features), BF16),
             pltpu.VMEM((2, LANES, HEAD_DIM), F32),
             pltpu.VMEM((2 * planes, 8, 128), F32),
+            pltpu.VMEM((8, 128), F32),
             pltpu.VMEM((planes, 2 * LANES, width), BF16),
             pltpu.VMEM((LANES, 512), F32),
             pltpu.VMEM((2, 2 * LANES, 512), F32),
@@ -762,10 +727,9 @@
             pltpu.VMEM((planes, LANES, width), F32),
             pltpu.VMEM((rows, features), BF16),
             pltpu.VMEM((rows, features), BF16),
-            pltpu.VMEM((planes, width, 256), BF16),
-            pltpu.VMEM((LANES, 256), BF16),
-            pltpu.VMEM((rows, 256), BF16),
-            pltpu.VMEM((planes, rows, width), BF16),
+            pltpu.VMEM((planes, width, 512), BF16),
+            pltpu.VMEM((2, LANES, 256), BF16),
+            pltpu.VMEM((2, rows, 256), BF16),
             dma((6,)),
             dma((14 + planes,)),
             dma((14 + planes,)),
@@ -777,14 +741,12 @@
             dma((8,)),
             dma((2, planes)),
             dma((2, planes)),
-            dma((planes,)),
-            dma((planes,)),
         ],
         compiler_params=pltpu.CompilerParams(
-            collective_id=0, has_side_effects=True, vmem_limit_bytes=67_043_328
+            collective_id=0, has_side_effects=True, vmem_limit_bytes=52 * 2**20
         ),
         name="tick",
-    )(xs[0], xf[0], dy[0], pos_tile, tables, gain, wq[0], wkv[0], wo[0])
+    )(xs[0], xf[0], dy[0], positions[None, :], frequency, gain, wq[0], wkv[0], wo[0])
     return produced[None], grads[None]
 
 

time: 167 us -> 159 us (0.952)
  Pallas kernels: 161 us -> 153 us
  other arithmetic: 1.7 us -> 0 us
    pallas_call x1, Pallas kernels: 161 us -> 153 us  [shards(): pl.pallas_call(functools.partial(tick, planes, rows), out_shape=(out, out...]
    unnamed x2 -> x12, local copies, waits for them, and re-layouts: 3.64 us -> 5.5 us
where the time goes in v4:
time: 159 us
  Pallas kernels  153 us (96%)
  local copies, waits for them, and re-layouts  5.5 us (3%)
    pallas_call x1, Pallas kernels, shards(): pl.pallas_call(functools.partial(tick, planes, rows), out_shape=(out, out...  153 us
    unnamed x12, local copies, waits for them, and re-layouts  5.5 us

profile of v4, /device:TPU:1, one launch (start us, length us, event | category | flops | bytes accessed | tf_op | source)
XLA Modules:
  0.0 159.1 jit_solution(17801466622600026972)
XLA Ops:
  0.6 0.0 copy-start
  0.6 1.0 copy-done
  1.7 0.0 copy-start.1
  1.7 0.9 copy-done.1
  2.6 0.0 copy-start.2
  2.6 0.7 copy-done.2
  3.3 0.0 copy-start.3
  3.3 0.7 copy-done.3
  4.0 0.0 copy-start.4
  4.0 0.7 copy-done.4
  4.6 152.9 %tick.1 = (bf16[112,2048]{1,0:T(8,128)(2,1)S(1)}, bf16[112,2048]{1,0:T(8,128)(2,1)S(1)}) custom-call(bf16[112,2048]{1,0:T(8,128)(2,1)S(1)} %bitcast.11, bf16[112,2048]{1,0:T(8,128)(2,1)} %bitcast.16, bf16[112,2048]{1,0:T(8,128)(2,1)} %bitcast.17, s32[1,112]{1,0:T(1,128)S(1)} %bitcast.13, f32[1,128]{1,0:T(1,128)S(1)} %copy-done.4, f32[1,2048]{1,0:T(1,128)S(1)} %copy-done.2, ...), custom_call_target="tpu_custom_call" | custom-call | tf_op jit(solution)/shard_map/tick/pallas_call | solution.py:695
  157.5 0.8 copy.13
  158.3 0.8 copy.14
Async XLA Ops:
  0.6 1.0 copy-start
  1.7 0.9 copy-start.1
  2.6 0.7 copy-start.2
  3.3 0.7 copy-start.3
  4.0 0.7 copy-start.4

commit v5 on v4

--- a/solution.py
+++ b/solution.py
@@ -189,7 +189,7 @@
         def copy(self, n, way, t):
             block = self.parts[n][0](plane(-t if way == 0 else t))
             sems = (self.number, n, way, t)
-            return remote(block, block, ring_send.at[sems], ring_recv.at[sems], ctx=to_z[way])
+            return remote(block, block, ring_send.at[self.number], ring_recv.at[sems], ctx=to_z[way])
 
         def step(self, t, ready=None, only=None):
             for n, (_, *hops) in enumerate(self.parts):
@@ -203,12 +203,6 @@
                     if t < hops[way]:
                         self.copy(n, way, t).start()
 
-        def sent(self):
-            for n, (_, *hops) in enumerate(self.parts):
-                for way in range(2):
-                    for t in range(hops[way]):
-                        self.copy(n, way, t).wait_send()
-
     def rows_of(ref, c):
         who = h if c == 0 else 1 - h
         at = pl.ds(pl.multiple_of(who * half, 128), half)
@@ -224,7 +218,8 @@
         return [(block(0), far, far - 1), (block(1), far - 1, far)]
 
     pos_part = (lambda p: posb.at[pl.ds(2 * p, 2)], far, far - 1)
-    ring_wkv = Ring(0, [*w_parts(wkvb), pos_part])
+    ring_wkv = Ring(0, w_parts(wkvb))
+    ring_pos = Ring(5, [pos_part])
     ring_q = [Ring(1 + j, w_parts(wqb.at[j])) for j in range(2)]
     ring_kv = [Ring(3 + m, kv_parts(m)) for m in range(2)]
 
@@ -235,8 +230,9 @@
         elif n == 1:
             swap[0].wait_recv()
             swap[1].wait_recv()
-        else:
-            swap[2].wait_recv()
+
+    def ready_pos(n):
+        swap[2].wait_recv()
 
     def ready_q(j):
         def ready(n):
@@ -382,7 +378,7 @@
 
     def rs_copy(j, k, way, t):
         at = (j, k, way, t)
-        return remote(stage.at[at], landed.at[at], rs_send.at[at], rs_recv.at[at], ctx=to_z[way])
+        return remote(stage.at[at], landed.at[at], rs_send.at[j], rs_recv.at[at], ctx=to_z[way])
 
     def rs_step(j, t):
         for k in range(2):
@@ -410,13 +406,16 @@
         ring_wkv.step(0, ready_wkv, 0)
         ring_q[0].step(0, ready_q(0), 0)
         ring_wkv.step(0, ready_wkv, 1)
-        ring_wkv.step(0, ready_wkv, 2)
+        ring_pos.step(0, ready_pos)
     with scope("a1"):
         ring_wkv.step(1)
+        ring_pos.step(1)
     with scope("a2"):
         ring_wkv.step(2)
+        ring_pos.step(2)
     with scope("a3"):
         ring_wkv.step(3)
+        ring_pos.step(3)
     with scope("c0"):
         ring_q[0].step(1, None, 0)
         ring_q[0].step(0, ready_q(0), 1)
@@ -426,6 +425,7 @@
         make_tables()
     with scope("a4"):
         ring_wkv.step(4)
+        ring_pos.step(4)
     for k in range(2):
         lend(k).start()
     with scope("kv0"):
@@ -626,7 +626,7 @@
     def out_copy(which, p):
         at = pl.ds(p * width, width)
         src, dst, to = ((fout, next_out, f_to), (gout, grad_out, g_to))[which]
-        return remote(src.at[:, at], dst.at[:, at], out_send.at[which, p], out_recv.at[which, p], **to)
+        return remote(src.at[:, at], dst.at[:, at], out_send.at[which], out_recv.at[which], **to)
 
     with scope("out"):
         for n in range(8):
@@ -666,19 +666,27 @@
     with scope("sent"):
         for c in (*swap, own_swap(0), own_swap(1), lend(0), lend(1), *(mix_copy(n) for n in range(8))):
             c.wait_send()
-        for ring in (ring_wkv, *ring_q, *ring_kv):
-            ring.sent()
-        for j in range(2):
-            for k in range(2):
-                for way in range(2):
-                    for t in range(rs_hops[k][way]):
-                        rs_copy(j, k, way, t).wait_send()
+        most = pl.ds(0, planes - 1)
+        many = pl.ds(0, (planes - 1) * pair)
+        whole = [
+            (wkvb.at[most], ring_send.at[0]),
+            (posb.at[pl.ds(0, 2 * planes - 2)], ring_send.at[5]),
+            (wqb.at[0, most], ring_send.at[1]),
+            (wqb.at[1, most], ring_send.at[2]),
+            (kv.at[0, :, :, many, :], ring_send.at[3]),
+            (kv.at[1, :, :, many, :], ring_send.at[4]),
+            (kv.at[0, 0, :, many, :], rs_send.at[0]),
+            (kv.at[0, 0, :, many, :], rs_send.at[1]),
+            (fout, out_send.at[0]),
+            (gout, out_send.at[1]),
+        ]
+        for ref, sem in whole:
+            remote(ref, ref, sem, sem, ctx=partner).wait_send()
         for p in range(planes):
             dn_copy(p).wait_send()
     with scope("outs"):
-        for which in range(2):
-            for p in range(planes):
-                out_copy(which, p).wait()
+        for which, (ref, out, to) in enumerate(((fout, next_out, f_to), (gout, grad_out, g_to))):
+            remote(ref, out, out_send.at[which], out_recv.at[which], **to).wait_recv()
 
 
 def shards(planes, xf, xs, dy, positions, gain, wq, wkv, wo):
@@ -733,14 +741,14 @@
             dma((6,)),
             dma((14 + planes,)),
             dma((14 + planes,)),
-            dma((5, 3, 2, far)),
-            dma((5, 3, 2, far)),
-            dma((2, 2, 2, far)),
+            dma((6,)),
+            dma((6, 2, 2, far)),
+            dma((2,)),
             dma((2, 2, 2, far)),
             dma((8,)),
             dma((8,)),
-            dma((2, planes)),
-            dma((2, planes)),
+            dma((2,)),
+            dma((2,)),
         ],
         compiler_params=pltpu.CompilerParams(
             collective_id=0, has_side_effects=True, vmem_limit_bytes=52 * 2**20

time: 159 us -> 158 us (level)
  Pallas kernels: 153 us -> 151 us
    pallas_call x1, Pallas kernels: 153 us -> 151 us  [shards(): pl.pallas_call(functools.partial(tick, planes, rows), out_shape=(out, out...]
where the time goes in v5:
time: 158 us; the launch traced here: 157 us
  Pallas kernels  151 us (96%)
  local copies, waits for them, and re-layouts  5.5 us (3%)
    pallas_call x1, Pallas kernels, shards(): pl.pallas_call(functools.partial(tick, planes, rows), out_shape=(out, out...  151 us
    unnamed x12, local copies, waits for them, and re-layouts  5.5 us

profile of v5, /device:TPU:1, one launch (start us, length us, event | category | flops | bytes accessed | tf_op | source)
XLA Modules:
  0.0 157.3 jit_solution(9681628663284811349)
XLA Ops:
  0.6 0.0 copy-start
  0.6 1.0 copy-done
  1.7 0.0 copy-start.1
  1.7 0.9 copy-done.1
  2.6 0.0 copy-start.2
  2.6 0.7 copy-done.2
  3.3 0.0 copy-start.3
  3.3 0.7 copy-done.3
  4.0 0.0 copy-start.4
  4.0 0.7 copy-done.4
  4.6 151.1 %tick.1 = (bf16[112,2048]{1,0:T(8,128)(2,1)S(1)}, bf16[112,2048]{1,0:T(8,128)(2,1)S(1)}) custom-call(bf16[112,2048]{1,0:T(8,128)(2,1)S(1)} %bitcast.11, bf16[112,2048]{1,0:T(8,128)(2,1)} %bitcast.16, bf16[112,2048]{1,0:T(8,128)(2,1)} %bitcast.17, s32[1,112]{1,0:T(1,128)S(1)} %bitcast.13, f32[1,128]{1,0:T(1,128)S(1)} %copy-done.4, f32[1,2048]{1,0:T(1,128)S(1)} %copy-done.2, ...), custom_call_target="tpu_custom_call" | custom-call | tf_op jit(solution)/shard_map/tick/pallas_call | solution.py:703
  155.8 0.8 copy.13
  156.5 0.8 copy.14
Async XLA Ops:
  0.6 1.0 copy-start
  1.7 0.9 copy-start.1
  2.6 0.7 copy-start.2
  3.3 0.7 copy-start.3
  4.0 0.7 copy-start.4
